TPU v7x, 128 devices: a whole 4x4x4 slice. The times are simulated.
128 devices in a mesh: dp: 8 (over x, core), mp: 16 (over y, z).
Axes of the slice: x: 4, y: 4, z: 4, core: 2. Of those that a mesh axis runs over, the one named last changes fastest.
Arguments:
- tokens: bfloat16 [256, 8192], P('dp', 'mp'), may hold values from -6 to 6
- gate_up_weight: bfloat16 [2, 8192, 15360], P(None, 'mp', 'dp'), may hold values from -0.0625 to 0.0625
- down_weight: bfloat16 [15360, 8192], P('dp', 'mp'), may hold values from -0.046875 to 0.046875
- gate_up_input_factor: bfloat16 [2, 8192, 64], P(None, 'mp'), may hold values from -0.0625 to 0.0625
- gate_up_output_factor: bfloat16 [2, 64, 15360], P(None, None, 'dp'), may hold values from -0.046875 to 0.046875
- down_input_factor: bfloat16 [15360, 64], P('dp'), may hold values from -0.046875 to 0.046875
- down_output_factor: bfloat16 [64, 8192], P(None, 'mp'), may hold values from -0.0625 to 0.0625
- cotangent: bfloat16 [256, 8192], P('dp', 'mp'), may hold values from -6 to 6
Outputs:
- output: bfloat16 [256, 8192], P('dp', 'mp')
- input_grad: bfloat16 [256, 8192], P('dp', 'mp')
- grad_gate_up_lower: float32 [2, 8192, 64], P(None, 'mp')
- gate_up_output_factor_gradient: float32 [2, 64, 15360], P(None, None, 'dp')
- down_input_factor_gradient: float32 [15360, 64], P('dp')
- down_output_factor_gradient: float32 [64, 8192], P(None, 'mp')
All inputs are finite; a program needn't handle non-finite values.
Results may differ from a plain program's by a relative error of at most 0.0065.
Values may be sent and summed in bfloat16 or wider, within the bound.
No kernel may reach another device: no remote copies, remote signals or barrier semaphores. Data moves between devices by JAX's collectives and lax.ppermute only.
A program may use at most 64 MiB of HBM per device.

v0:
```python
import jax
import jax.numpy as jnp
from jax import lax
from jax.experimental import pallas as pl
from jax.experimental.pallas import tpu as pltpu
from jax.sharding import Mesh
from jax.sharding import PartitionSpec as P

F32 = jnp.float32
BF16 = jnp.bfloat16
adapter_scale = 2.0
CUT = 896


def other_core(x):
    return lax.ppermute(x, "dp", [(i, i ^ 1) for i in range(lax.axis_size("dp"))])


def to_chip(x, by):
    n = lax.axis_size("dp")
    return lax.ppermute(x, "dp", [(i, (i + 2 * by) % n) for i in range(n)])


def dot(a, b, dims=((1,), (0,))):
    return lax.dot_general(a, b, (dims, ((), ())), preferred_element_type=F32)


def along(x, stage, by):
    pairs = []
    for dp in range(8):
        for y in range(4):
            for z in range(4):
                if (dp + stage) % 2 == 0:
                    there = (y + by) % 4 * 4 + z
                else:
                    there = y * 4 + (z + by) % 4
                pairs.append((dp * 16 + y * 4 + z, dp * 16 + there))
    return lax.ppermute(x, ("dp", "y", "z"), pairs)


def exchanged(blocks, stage):
    return [
        blocks[0],
        along(blocks[1], stage, 1),
        along(blocks[3], stage, -1),
        along(blocks[2], stage, 2),
    ]


def collected(block, stage):
    return [block, along(block, stage, -1), along(block, stage, 2), along(block, stage, 1)]


def whole(n):
    return [pl.BlockSpec(memory_space=pltpu.VMEM)] * n


def in_vmem(shape, dtype):
    return pltpu.VMEM(shape, dtype)


T = ((1,), (1,))


def tiles(lo, hi, step=384):
    return [(a, min(a + step, hi)) for a in range(lo, hi, step)]


def store_blocks(outs, at, value):
    for k in range(4):
        rows = value[64 * k : 64 * k + 64].astype(outs[k].dtype)
        outs[k][:, at : at + value.shape[1]] = rows


def pack_kernel(tokens, cotangent, out, sems):
    copies = [
        pltpu.make_async_copy(tokens, out.at[:, :512], sems.at[0]),
        pltpu.make_async_copy(cotangent, out.at[:, 512:], sems.at[1]),
    ]
    for copy in copies:
        copy.start()
    for copy in copies:
        copy.wait()


def packed(tokens, cotangent):
    return pl.pallas_call(
        pack_kernel,
        out_shape=in_vmem((32, 1024), BF16),
        in_specs=[pl.BlockSpec(memory_space=pltpu.HBM)] * 2,
        out_specs=whole(1)[0],
        scratch_shapes=[pltpu.SemaphoreType.DMA((2,))],
        compiler_params=pltpu.CompilerParams(vmem_limit_bytes=2**20),
        cost_estimate=pl.CostEstimate(flops=10**6, bytes_accessed=10**5, transcendentals=0),
    )(tokens, cotangent)


def load_kernel(*refs):
    n = len(refs) // 2
    copies = [pltpu.make_async_copy(refs[k], refs[n + k], refs[-1].at[k]) for k in range(n)]
    for copy in copies:
        copy.start()
    for copy in copies:
        copy.wait()


def loaded(*arrays):
    return pl.pallas_call(
        load_kernel,
        out_shape=[in_vmem(a.shape, a.dtype) for a in arrays],
        in_specs=[pl.BlockSpec(memory_space=pltpu.HBM)] * len(arrays),
        out_specs=whole(len(arrays)),
        scratch_shapes=[pltpu.SemaphoreType.DMA((len(arrays),))],
        compiler_params=pltpu.CompilerParams(vmem_limit_bytes=2**20),
        cost_estimate=cost(2 * 10**9),
    )(*arrays)


def first_kernel(turn, near, wgu, wd, a_both, dof, rows, *outs):
    rows[...] = dot(turn[...], near[...]).astype(BF16)
    x, c = rows[:, :512], rows[:, 512:]
    store_blocks(outs, 0, dot(x, a_both[...], T))
    store_blocks(outs, 128, dot(c, dof[...], T))
    store_blocks(outs, 192, jnp.zeros((256, 64), F32))
    for k in range(2):
        for lo, hi in tiles(0, CUT):
            store_blocks(outs, 256 + k * CUT + lo, dot(x, wgu[k, :, lo:hi]))
    for lo, hi in tiles(0, CUT):
        store_blocks(outs, 256 + 2 * CUT + lo, dot(c, wd[lo:hi, :], T))


def first_half(turn, near, wgu, wd, a_both, dof):
    shape = (64, 256 + 3 * CUT)
    return pl.pallas_call(
        first_kernel,
        out_shape=[in_vmem((256, 1024), BF16), in_vmem(shape, F32)] + [in_vmem(shape, BF16)] * 3,
        in_specs=whole(6),
        out_specs=whole(5),
        compiler_params=pltpu.CompilerParams(vmem_limit_bytes=12 * 2**20),
        cost_estimate=pl.CostEstimate(flops=10**9, bytes_accessed=10**6, transcendentals=0),
    )(turn, near, wgu, wd, a_both, dof)


def second_kernel(rows, wgu, wd, *outs):
    x, c = rows[:, :512], rows[:, 512:]
    n = 1920 - CUT
    for k in range(2):
        for lo, hi in tiles(CUT, 1920):
            store_blocks(outs, k * n + lo - CUT, dot(x, wgu[k, :, lo:hi]))
    for lo, hi in tiles(CUT, 1920):
        store_blocks(outs, 2 * n + lo - CUT, dot(c, wd[lo:hi, :], T))


def second_half(rows, wgu, wd):
    shape = (64, 3 * (1920 - CUT))
    return pl.pallas_call(
        second_kernel,
        out_shape=[in_vmem(shape, F32)] + [in_vmem(shape, BF16)] * 3,
        in_specs=whole(3),
        out_specs=whole(4),
        compiler_params=pltpu.CompilerParams(vmem_limit_bytes=12 * 2**20),
        cost_estimate=pl.CostEstimate(flops=10**9, bytes_accessed=10**6, transcendentals=0),
    )(rows, wgu, wd)


def params(mib=12):
    return pltpu.CompilerParams(vmem_limit_bytes=mib * 2**20)


def cost(flops):
    return pl.CostEstimate(flops=flops, bytes_accessed=10**6, transcendentals=0)


def total(refs):
    return (
        refs[0][...].astype(F32)
        + refs[1][...].astype(F32)
        + refs[2][...].astype(F32)
        + refs[3][...].astype(F32)
    )


def sum_kernel(*refs):
    value = total(refs[:4])
    for k in range(4):
        out = refs[4 + k]
        out[...] = value[16 * k : 16 * k + 16].astype(out.dtype)


def summed(blocks):
    shape = (16, blocks[0].shape[1])
    return pl.pallas_call(
        sum_kernel,
        out_shape=[in_vmem(shape, F32)] + [in_vmem(shape, BF16)] * 3,
        in_specs=whole(4),
        out_specs=whole(4),
        compiler_params=params(),
        cost_estimate=cost(10**7),
    )(*blocks)


def middle(low, back_down, value, at, lo, hi, bo, dif, out):
    w = hi - lo
    low = low.astype(BF16)
    gate = value[:, at : at + w] + adapter_scale * dot(low[:, :64], bo[0, :, lo:hi])
    up = value[:, at + w : at + 2 * w] + adapter_scale * dot(low[:, 64:], bo[1, :, lo:hi])
    back = value[:, at + 2 * w :] + adapter_scale * dot(back_down, dif[:, lo:hi])
    s = jax.nn.sigmoid(gate)
    out[:, at : at + w] = (gate * s * up).astype(BF16)
    out[:, at + w : at + 2 * w] = (back * up * s * (1.0 + gate * (1.0 - s))).astype(BF16)
    out[:, at + 2 * w :] = (back * gate * s).astype(BF16)


def middle_first_kernel(a, b, c, d, bo, dif, out):
    value = total((a, b, c, d))
    small = value[:, :256].astype(BF16)
    out[:, :256] = small
    middle(value[:, :128], small[:, 128:192], value, 256, 0, CUT, bo, dif, out)


def middle_second_kernel(a, b, c, d, first, bo, dif, out):
    value = total((a, b, c, d))
    middle(first[:, :128], first[:, 128:192], value, 0, CUT, 1920, bo, dif, out)


def middles(blocks, bo, dif, first=None):
    more = [] if first is None else [first]
    return pl.pallas_call(
        middle_first_kernel if first is None else middle_second_kernel,
        out_shape=in_vmem(blocks[0].shape, BF16),
        in_specs=whole(6 + len(more)),
        out_specs=whole(1)[0],
        compiler_params=params(),
        cost_estimate=cost(10**8),
    )(*blocks, *more, bo, dif)


def stack_kernel(a, b, c, d, out):
    for k, ref in enumerate((a, b, c, d)):
        out[16 * k : 16 * k + 16] = ref[...]


def stacked(blocks):
    return pl.pallas_call(
        stack_kernel,
        out_shape=in_vmem((64, blocks[0].shape[1]), BF16),
        in_specs=whole(4),
        out_specs=whole(1)[0],
        compiler_params=params(),
        cost_estimate=cost(10**7),
    )(*blocks)


def joined(refs, lo, hi):
    return jnp.concatenate([ref[:, lo:hi] for ref in refs], 0)


def factor_kernel(*refs):
    a, b, bo_grad, dif_grad = refs[:4], refs[4:8], refs[8], refs[9]
    n = ((0,), (0,))
    scale = adapter_scale * 256 ** (-0.5)
    small = joined(a, 0, 256)
    low, back_down = small[:, :128], small[:, 128:192]
    for part, at, lo, hi in ((a, 256, 0, CUT), (b, 0, CUT, 1920)):
        w = hi - lo
        dif_grad[:, lo:hi] = scale * dot(back_down, joined(part, at, at + w), n)
        for k in range(2):
            g = joined(part, at + (k + 1) * w, at + (k + 2) * w)
            bo_grad[k, :, lo:hi] = scale * dot(low[:, 64 * k : 64 * k + 64], g, n)


def factor_gradients(a, b):
    return pl.pallas_call(
        factor_kernel,
        out_shape=[
            jax.ShapeDtypeStruct((2, 64, 1920), F32),
            jax.ShapeDtypeStruct((64, 1920), F32),
        ],
        in_specs=whole(8),
        out_specs=whole(2),
        compiler_params=params(16),
        cost_estimate=cost(4 * 10**9),
    )(*a, *b)


def back_products(g, at, lo, hi, wgu, wd, bo, dif):
    w = hi - lo
    hidden, gate, up = (joined(g, at + k * w, at + (k + 1) * w) for k in range(3))
    return (
        dot(gate, bo[0, :, lo:hi], T),
        dot(up, bo[1, :, lo:hi], T),
        dot(hidden, dif[:, lo:hi], T),
        dot(hidden, wd[lo:hi, :]),
        dot(gate, wgu[0, :, lo:hi], T) + dot(up, wgu[1, :, lo:hi], T),
    )


def third_kernel(a, b, c, d, wgu, wd, bo, dif, small, out, grad):
    bl0, bl1, ld, o, g = back_products((a, b, c, d), 256, 0, CUT, wgu, wd, bo, dif)
    small[:, :64] = bl0
    small[:, 64:128] = bl1
    small[:, 128:192] = ld
    out[...] = o
    grad[...] = g


def third_half(g, wgu, wd, bo, dif):
    return pl.pallas_call(
        third_kernel,
        out_shape=[
            in_vmem((256, 256), F32),
            in_vmem((256, 512), F32),
            in_vmem((256, 512), F32),
        ],
        in_specs=whole(8),
        out_specs=whole(3),
        compiler_params=params(),
        cost_estimate=cost(10**9),
    )(*g, wgu, wd, bo, dif)


def fourth_kernel(a, b, c, d, wgu, wd, bo, dif, dof, turn, small, out, grad, mine, theirs):
    bl0, bl1, ld, o, g = back_products((a, b, c, d), 0, CUT, 1920, wgu, wd, bo, dif)
    low_down = small[:, 128:192] + ld
    o = o + out[...] + adapter_scale * dot(low_down.astype(BF16), dof[...])

    def put(value, at):
        value = dot(turn[...], value.astype(BF16), ((0,), (0,)))
        for k in range(4):
            mine[k, :, at : at + value.shape[1]] = value[64 * k : 64 * k + 32]
            theirs[k, :, at : at + value.shape[1]] = value[64 * k + 32 : 64 * k + 64].astype(BF16)

    put(small[:, :64] + bl0, 0)
    put(small[:, 64:128] + bl1, 64)
    put(low_down, 128)
    put(jnp.zeros((256, 64), F32), 192)
    put(o, 256)
    put(g + grad[...], 768)


def fourth_half(g, wgu, wd, bo, dif, dof, turn, small, out, grad):
    shape = (4, 32, 1280)
    return pl.pallas_call(
        fourth_kernel,
        out_shape=[in_vmem(shape, F32), in_vmem(shape, BF16)],
        in_specs=whole(13),
        out_specs=whole(2),
        compiler_params=params(),
        cost_estimate=cost(10**9),
    )(*g, wgu, wd, bo, dif, dof, turn, small, out, grad)


def core_sum_kernel(mine, theirs, own, one, two, three):
    value = [mine[k] + theirs[k].astype(F32) for k in range(4)]
    own[:, :1024] = value[0][:, 256:]
    for j in range(4):
        own[:, 1024 + 256 * j : 1280 + 256 * j] = value[j][:, :256]
    value = [v.astype(BF16) for v in value]
    for k, out in ((1, one), (2, two), (3, three)):
        out[:, :1024] = value[k][:, 256:]
        for j in range(4):
            out[:, 1024 + 256 * j : 1280 + 256 * j] = value[(j + k) % 4][:, :256]


def core_sums(mine, theirs):
    shape = (32, 2048)
    return pl.pallas_call(
        core_sum_kernel,
        out_shape=[in_vmem(shape, F32)] + [in_vmem(shape, BF16)] * 3,
        in_specs=whole(2),
        out_specs=whole(4),
        compiler_params=params(),
        cost_estimate=cost(10**7),
    )(mine, theirs)


def chip_sum_kernel(own, a, b, c, small, large):
    value = (
        own[...].astype(F32) + a[...].astype(F32) + b[...].astype(F32) + c[...].astype(F32)
    )
    large[...] = value[:, :1024]
    for j in range(4):
        small[j] = value[:, 1024 + 256 * j : 1280 + 256 * j].astype(BF16)


def chip_sums(own, got):
    return pl.pallas_call(
        chip_sum_kernel,
        out_shape=[in_vmem((4, 32, 256), BF16), in_vmem((32, 1024), F32)],
        in_specs=whole(4),
        out_specs=whole(2),
        compiler_params=params(),
        cost_estimate=cost(10**7),
    )(own, *got)


def finish_kernel(mine, theirs, large, near, a_both, output, input_grad, lower, dof_grad):
    n = ((0,), (0,))
    scale = adapter_scale * 256 ** (-0.5)
    small = jnp.concatenate([r for k in range(4) for r in (mine[k], theirs[k])], 0)
    lower[...] = scale * dot(small[:, :128], near[:, :512], n)
    dof_grad[...] = scale * dot(small[:, 128:192], near[:, 512:], n)
    output[...] = large[:, :512].astype(BF16)
    low = dot(mine[0, :, :128], a_both[...])
    input_grad[...] = (large[:, 512:] + adapter_scale * low).astype(BF16)


def finished(mine, theirs, large, near, a_both):
    return pl.pallas_call(
        finish_kernel,
        out_shape=[
            jax.ShapeDtypeStruct((32, 512), BF16),
            jax.ShapeDtypeStruct((32, 512), BF16),
            jax.ShapeDtypeStruct((128, 512), F32),
            jax.ShapeDtypeStruct((64, 512), F32),
        ],
        in_specs=whole(5),
        out_specs=whole(4),
        compiler_params=params(),
        cost_estimate=cost(10**8),
    )(mine, theirs, large, near, a_both)


def on_device(
    tokens,
    gate_up_weight,
    down_weight,
    gate_up_input_factor,
    gate_up_output_factor,
    down_input_factor,
    down_output_factor,
    cotangent,
):
    dp = lax.axis_index("dp")
    chip, core = dp // 2, dp % 2
    y, z = lax.axis_index("y"), lax.axis_index("z")

    mine = packed(tokens, cotangent)
    a_raw = gate_up_input_factor.transpose(0, 2, 1).reshape(128, 512)
    pair = jnp.concatenate([mine, other_core(mine)], 0)
    near = [pair, to_chip(pair, -1), to_chip(pair, 2), to_chip(pair, 1)]
    near = jnp.concatenate(near, 0)
    wgu1, wd1, a_both, dof = loaded(
        gate_up_weight, down_weight, a_raw, down_output_factor
    )

    n = jnp.arange(256, dtype=jnp.int32)
    first, second = n // 64, n // 16 % 4
    y_by, z_by = jnp.where(core == 0, first, second), jnp.where(core == 0, second, first)
    token_of_row = 64 * ((y + y_by) % 4) + 16 * ((z + z_by) % 4) + n % 16
    token_of_near = 64 * ((chip + n // 64) % 4) + 32 * (core ^ (n // 32 % 2)) + n % 32
    turn = (token_of_row[:, None] == token_of_near[None, :]).astype(BF16)
    wgu, wd, bo, dif = gate_up_weight, down_weight, gate_up_output_factor, down_input_factor.T
    rows, *part_a = first_half(turn, near, wgu1, wd1, a_both, dof)
    part_b = second_half(rows, wgu1, wd1)
    half_a = summed(exchanged(part_a, 0))
    half_b = summed(exchanged(part_b, 0))
    mid_a = middles(exchanged(half_a, 1), bo, dif)
    mid_b = middles(exchanged(half_b, 1), bo, dif, mid_a)
    all_a = collected(stacked(collected(mid_a, 1)), 0)
    all_b = collected(stacked(collected(mid_b, 1)), 0)

    halves = third_half(all_a, wgu, wd, bo, dif)
    sums, sent = fourth_half(all_b, wgu, wd, bo, dif, down_output_factor, turn, *halves)
    arrived = other_core(sent)
    *everything, arrived = lax.optimization_barrier((*all_a, *all_b, arrived))
    gate_up_output_factor_gradient, down_input_factor_gradient = factor_gradients(
        everything[:4], everything[4:]
    )
    own, *sent = core_sums(sums, arrived)
    got = [to_chip(sent[0], 1), to_chip(sent[2], 3), to_chip(sent[1], 2)]
    small, large = chip_sums(own, got)
    output, input_grad, lower, down_output_factor_gradient = finished(
        small, other_core(small), large, near, a_raw
    )
    grad_gate_up_lower = lower.reshape(2, 64, 512).transpose(0, 2, 1)
    return (
        output,
        input_grad,
        grad_gate_up_lower,
        gate_up_output_factor_gradient,
        down_input_factor_gradient.T,
        down_output_factor_gradient,
    )


def solution(mesh):
    torus = Mesh(mesh.devices.reshape(mesh.shape["dp"], 4, 4), ("dp", "y", "z"))
    mp = ("y", "z")
    in_specs = (
        P("dp", mp),
        P(None, mp, "dp"),
        P("dp", mp),
        P(None, mp, None),
        P(None, None, "dp"),
        P("dp", None),
        P(None, mp),
        P("dp", mp),
    )
    out_specs = (
        P("dp", mp),
        P("dp", mp),
        P(None, mp, None),
        P(None, None, "dp"),
        P("dp", None),
        P(None, mp),
    )
    return jax.shard_map(
        on_device, mesh=torus, in_specs=in_specs, out_specs=out_specs, check_vma=False
    )
```

profile of v0, /device:TPU:0, one launch (start us, length us, event | category | flops | bytes accessed | tf_op | source)
XLA Modules:
  0.0 116.0 jit_solution(4519083296074335641)
XLA Ops:
  2.4 2.1 %copy-done = bf16[2,512,1920]{2,1,0:T(8,128)(2,1)S(1)} copy-done((bf16[2,512,1920]{2,1,0:T(8,128)(2,1)S(1)}, bf16[2,512,1920]{2,1,0:T(8,128)(2,1)}, u32[]{:S(2)}) %copy-start) | copy-done | bytes 3932184
  4.6 1.5 %copy-done.2 = bf16[1920,512]{1,0:T(8,128)(2,1)S(1)} copy-done((bf16[1920,512]{1,0:T(8,128)(2,1)S(1)}, bf16[1920,512]{1,0:T(8,128)(2,1)}, u32[]{:S(2)}) %copy-start.2) | copy-done | bytes 1966104
  8.7 2.9 %collective-permute-start.1 = (bf16[64,1024]{1,0:T(8,128)(2,1)S(1)}, bf16[64,1024]{1,0:T(8,128)(2,1)S(1)}, u32[]{:S(2)}, u32[]{:S(2)}) collective-permute-start(bf16[64,1024]{1,0:T(8,128)(2,1)S(1)} %pad_maximum_fusion), channel_id=1, source_target_pairs={{0,96},{16,112},{32,0},{48,16},{64,32},{80,48},{96,64},{112,80},{1... | collective-permute-start | bytes 393224 | tf_op jit(solution)/shard_map/ppermute | solution.py:21
  11.7 2.3 %collective-permute-start.2 = (bf16[64,1024]{1,0:T(8,128)(2,1)S(1)}, bf16[64,1024]{1,0:T(8,128)(2,1)S(1)}, u32[]{:S(2)}, u32[]{:S(2)}) collective-permute-start(bf16[64,1024]{1,0:T(8,128)(2,1)S(1)} %pad_maximum_fusion), channel_id=1, source_target_pairs={{0,64},{16,80},{32,96},{48,112},{64,0},{80,16},{96,32},{112,48},{1... | collective-permute-start | bytes 393224 | tf_op jit(solution)/shard_map/ppermute | solution.py:21
  15.1 5.4 %collective-permute-done.2 = bf16[64,1024]{1,0:T(8,128)(2,1)S(1)} collective-permute-done((bf16[64,1024]{1,0:T(8,128)(2,1)S(1)}, bf16[64,1024]{1,0:T(8,128)(2,1)S(1)}, u32[]{:S(2)}, u32[]{:S(2)}) %collective-permute-start.2) | collective-permute-done | bytes 131104 | tf_op jit(solution)/shard_map/ppermute | solution.py:21
  21.3 1.5 %shard_map.129 = (bf16[256,1024]{1,0:T(8,128)(2,1)S(1)}, f32[64,2944]{1,0:T(8,128)S(1)}, bf16[64,2944]{1,0:T(8,128)(2,1)S(1)}, bf16[64,2944]{1,0:T(8,128)(2,1)S(1)}, bf16[64,2944]{1,0:T(8,128)(2,1)S(1)}) custom-call(bf16[256,256]{1,0:T(8,128)(2,1)S(1)} %compare_convert_fusion.turn, bf16[256,1024]{1,0:T(8,128)(2,1)S(1)} %constant_dynamic-update-slice_fusion.near, ...), custom_call_target="tpu_custom_call" | custom-call | flops 1000000000 | bytes 1000000 | tf_op jit(solution)/shard_map/pallas_call | solution.py:134
  22.8 1.6 %collective-permute-start.10 = (bf16[64,2944]{1,0:T(8,128)(2,1)S(1)}, bf16[64,2944]{1,0:T(8,128)(2,1)S(1)}, u32[]{:S(2)}, u32[]{:S(2)}) collective-permute-start(bf16[64,2944]{1,0:T(8,128)(2,1)S(1)} %get-tuple-element.67), channel_id=1, source_target_pairs={{0,4},{1,5},{2,6},{3,7},{4,8},{5,9},{6,10},{7,11},{8,12},{9,13},{1... | collective-permute-start | bytes 1130504 | tf_op jit(solution)/shard_map/ppermute | solution.py:38
  24.5 1.7 %collective-permute-start.11 = (bf16[64,2944]{1,0:T(8,128)(2,1)S(1)}, bf16[64,2944]{1,0:T(8,128)(2,1)S(1)}, u32[]{:S(2)}, u32[]{:S(2)}) collective-permute-start(bf16[64,2944]{1,0:T(8,128)(2,1)S(1)} %get-tuple-element.68), channel_id=1, source_target_pairs={{0,12},{1,13},{2,14},{3,15},{4,0},{5,1},{6,2},{7,3},{8,4},{9,5},{1... | collective-permute-start | bytes 1130504 | tf_op jit(solution)/shard_map/ppermute | solution.py:38
  26.1 2.0 %collective-permute-start.12 = (bf16[64,2944]{1,0:T(8,128)(2,1)S(1)}, bf16[64,2944]{1,0:T(8,128)(2,1)S(1)}, u32[]{:S(2)}, u32[]{:S(2)}) collective-permute-start(bf16[64,2944]{1,0:T(8,128)(2,1)S(1)} %get-tuple-element.69), channel_id=1, source_target_pairs={{0,8},{1,9},{2,10},{3,11},{4,12},{5,13},{6,14},{7,15},{8,0},{9,1},... | collective-permute-start | bytes 1130504 | tf_op jit(solution)/shard_map/ppermute | solution.py:38
  28.1 3.6 %collective-permute-done.10.refs_1_ = bf16[64,2944]{1,0:T(8,128)(2,1)S(1)} collective-permute-done((bf16[64,2944]{1,0:T(8,128)(2,1)S(1)}, bf16[64,2944]{1,0:T(8,128)(2,1)S(1)}, u32[]{:S(2)}, u32[]{:S(2)}) %collective-permute-start.10) | collective-permute-done | bytes 376864 | tf_op jit(solution)/shard_map/ppermute | solution.py:38
  32.1 4.9 %collective-permute-done.12.refs_3_ = bf16[64,2944]{1,0:T(8,128)(2,1)S(1)} collective-permute-done((bf16[64,2944]{1,0:T(8,128)(2,1)S(1)}, bf16[64,2944]{1,0:T(8,128)(2,1)S(1)}, u32[]{:S(2)}, u32[]{:S(2)}) %collective-permute-start.12) | collective-permute-done | bytes 376864 | tf_op jit(solution)/shard_map/ppermute | solution.py:38
  37.1 2.0 %collective-permute-start.13 = (bf16[16,2944]{1,0:T(8,128)(2,1)S(1)}, bf16[16,2944]{1,0:T(8,128)(2,1)S(1)}, u32[]{:S(2)}, u32[]{:S(2)}) collective-permute-start(bf16[16,2944]{1,0:T(8,128)(2,1)S(1)} %get-tuple-element.71), channel_id=1, source_target_pairs={{0,1},{1,2},{2,3},{3,0},{4,5},{5,6},{6,7},{7,4},{8,9},{9,10},{10,1... | collective-permute-start | bytes 282632 | tf_op jit(solution)/shard_map/ppermute | solution.py:38
  41.8 1.8 %collective-permute-start.5 = (bf16[64,3072]{1,0:T(8,128)(2,1)S(1)}, bf16[64,3072]{1,0:T(8,128)(2,1)S(1)}, u32[]{:S(2)}, u32[]{:S(2)}) collective-permute-start(bf16[64,3072]{1,0:T(8,128)(2,1)S(1)} %get-tuple-element.60), channel_id=1, source_target_pairs={{0,12},{1,13},{2,14},{3,15},{4,0},{5,1},{6,2},{7,3},{8,4},{9,5},{1... | collective-permute-start | bytes 1179656 | tf_op jit(solution)/shard_map/ppermute | solution.py:38
  44.0 2.1 %collective-permute-start.14 = (bf16[16,2944]{1,0:T(8,128)(2,1)S(1)}, bf16[16,2944]{1,0:T(8,128)(2,1)S(1)}, u32[]{:S(2)}, u32[]{:S(2)}) collective-permute-start(bf16[16,2944]{1,0:T(8,128)(2,1)S(1)} %get-tuple-element.72), channel_id=1, source_target_pairs={{0,3},{1,0},{2,1},{3,2},{4,7},{5,4},{6,5},{7,6},{8,11},{9,8},{10,9... | collective-permute-start | bytes 282632 | tf_op jit(solution)/shard_map/ppermute | solution.py:38
  46.1 1.9 %collective-permute-start.15 = (bf16[16,2944]{1,0:T(8,128)(2,1)S(1)}, bf16[16,2944]{1,0:T(8,128)(2,1)S(1)}, u32[]{:S(2)}, u32[]{:S(2)}) collective-permute-start(bf16[16,2944]{1,0:T(8,128)(2,1)S(1)} %get-tuple-element.73), channel_id=1, source_target_pairs={{0,2},{1,3},{2,0},{3,1},{4,6},{5,7},{6,4},{7,5},{8,10},{9,11},{10,... | collective-permute-start | bytes 282632 | tf_op jit(solution)/shard_map/ppermute | solution.py:38
  48.0 4.6 %collective-permute-done.14.c = bf16[16,2944]{1,0:T(8,128)(2,1)S(1)} collective-permute-done((bf16[16,2944]{1,0:T(8,128)(2,1)S(1)}, bf16[16,2944]{1,0:T(8,128)(2,1)S(1)}, u32[]{:S(2)}, u32[]{:S(2)}) %collective-permute-start.14) | collective-permute-done | bytes 94240 | tf_op jit(solution)/shard_map/ppermute | solution.py:38
  54.9 3.1 %collective-permute-start.23 = (bf16[16,2944]{1,0:T(8,128)(2,1)S(1)}, bf16[16,2944]{1,0:T(8,128)(2,1)S(1)}, u32[]{:S(2)}, u32[]{:S(2)}) collective-permute-start(bf16[16,2944]{1,0:T(8,128)(2,1)S(1)} %shard_map.133.first.a), channel_id=1, source_target_pairs={{0,2},{1,3},{2,0},{3,1},{4,6},{5,7},{6,4},{7,5},{8,10},{9,11},{10,... | collective-permute-start | bytes 282632 | tf_op jit(solution)/shard_map/ppermute | solution.py:38
  59.3 1.8 %collective-permute-start.22 = (bf16[16,2944]{1,0:T(8,128)(2,1)S(1)}, bf16[16,2944]{1,0:T(8,128)(2,1)S(1)}, u32[]{:S(2)}, u32[]{:S(2)}) collective-permute-start(bf16[16,2944]{1,0:T(8,128)(2,1)S(1)} %shard_map.133.first.a), channel_id=1, source_target_pairs={{0,3},{1,0},{2,1},{3,2},{4,7},{5,4},{6,5},{7,6},{8,11},{9,8},{10,9... | collective-permute-start | bytes 282632 | tf_op jit(solution)/shard_map/ppermute | solution.py:38
  61.5 2.3 %collective-permute-done.22.b = bf16[16,2944]{1,0:T(8,128)(2,1)S(1)} collective-permute-done((bf16[16,2944]{1,0:T(8,128)(2,1)S(1)}, bf16[16,2944]{1,0:T(8,128)(2,1)S(1)}, u32[]{:S(2)}, u32[]{:S(2)}) %collective-permute-start.22) | collective-permute-done | bytes 94240 | tf_op jit(solution)/shard_map/ppermute | solution.py:38
  65.7 3.2 %collective-permute-start.8 = (bf16[16,3072]{1,0:T(8,128)(2,1)S(1)}, bf16[16,3072]{1,0:T(8,128)(2,1)S(1)}, u32[]{:S(2)}, u32[]{:S(2)}) collective-permute-start(bf16[16,3072]{1,0:T(8,128)(2,1)S(1)} %get-tuple-element.64), channel_id=1, source_target_pairs={{0,3},{1,0},{2,1},{3,2},{4,7},{5,4},{6,5},{7,6},{8,11},{9,8},{10,9... | collective-permute-start | bytes 294920 | tf_op jit(solution)/shard_map/ppermute | solution.py:38
  71.4 3.6 %collective-permute-done.9.d = bf16[16,3072]{1,0:T(8,128)(2,1)S(1)} collective-permute-done((bf16[16,3072]{1,0:T(8,128)(2,1)S(1)}, bf16[16,3072]{1,0:T(8,128)(2,1)S(1)}, u32[]{:S(2)}, u32[]{:S(2)}) %collective-permute-start.9) | collective-permute-done | bytes 98336 | tf_op jit(solution)/shard_map/ppermute | solution.py:38
  75.7 3.1 %collective-permute-start.17 = (bf16[16,3072]{1,0:T(8,128)(2,1)S(1)}, bf16[16,3072]{1,0:T(8,128)(2,1)S(1)}, u32[]{:S(2)}, u32[]{:S(2)}) collective-permute-start(bf16[16,3072]{1,0:T(8,128)(2,1)S(1)} %shard_map.134.a), channel_id=1, source_target_pairs={{0,2},{1,3},{2,0},{3,1},{4,6},{5,7},{6,4},{7,5},{8,10},{9,11},{10,... | collective-permute-start | bytes 294920 | tf_op jit(solution)/shard_map/ppermute | solution.py:38
  79.4 1.8 %collective-permute-start.26 = (bf16[64,2944]{1,0:T(8,128)(2,1)S(1)}, bf16[64,2944]{1,0:T(8,128)(2,1)S(1)}, u32[]{:S(2)}, u32[]{:S(2)}) collective-permute-start(bf16[64,2944]{1,0:T(8,128)(2,1)S(1)} %shard_map.136.a.refs_0_), channel_id=1, source_target_pairs={{0,8},{1,9},{2,10},{3,11},{4,12},{5,13},{6,14},{7,15},{8,0},{9,1},... | collective-permute-start | bytes 1130504 | tf_op jit(solution)/shard_map/ppermute | solution.py:38
  86.6 2.0 %collective-permute-start.20 = (bf16[64,3072]{1,0:T(8,128)(2,1)S(1)}, bf16[64,3072]{1,0:T(8,128)(2,1)S(1)}, u32[]{:S(2)}, u32[]{:S(2)}) collective-permute-start(bf16[64,3072]{1,0:T(8,128)(2,1)S(1)} %shard_map.135.a.refs_4_), channel_id=1, source_target_pairs={{0,8},{1,9},{2,10},{3,11},{4,12},{5,13},{6,14},{7,15},{8,0},{9,1},... | collective-permute-start | bytes 1179656 | tf_op jit(solution)/shard_map/ppermute | solution.py:38
  88.6 1.6 %collective-permute-start.19 = (bf16[64,3072]{1,0:T(8,128)(2,1)S(1)}, bf16[64,3072]{1,0:T(8,128)(2,1)S(1)}, u32[]{:S(2)}, u32[]{:S(2)}) collective-permute-start(bf16[64,3072]{1,0:T(8,128)(2,1)S(1)} %shard_map.135.a.refs_4_), channel_id=1, source_target_pairs={{0,12},{1,13},{2,14},{3,15},{4,0},{5,1},{6,2},{7,3},{8,4},{9,5},{1... | collective-permute-start | bytes 1179656 | tf_op jit(solution)/shard_map/ppermute | solution.py:38
  94.3 4.3 %collective-permute-done.20.c.refs_6_ = bf16[64,3072]{1,0:T(8,128)(2,1)S(1)} collective-permute-done((bf16[64,3072]{1,0:T(8,128)(2,1)S(1)}, bf16[64,3072]{1,0:T(8,128)(2,1)S(1)}, u32[]{:S(2)}, u32[]{:S(2)}) %collective-permute-start.20) | collective-permute-done | bytes 393248 | tf_op jit(solution)/shard_map/ppermute | solution.py:38
  100.0 1.7 %shard_map.138 = (f32[4,32,1280]{2,1,0:T(8,128)S(1)}, bf16[4,32,1280]{2,1,0:T(8,128)(2,1)S(1)}) custom-call(bf16[64,3072]{1,0:T(8,128)(2,1)S(1)} %shard_map.135.a.refs_4_, bf16[64,3072]{1,0:T(8,128)(2,1)S(1)} %collective-permute-done.19.b.refs_5_, bf16[64,3072]{1,0:T(8,128)(2,1)S(1)} %collective-permute-done.20.c.refs_6_, ...), custom_call_target="tpu_custom_call" | custom-call | flops 1000000000 | bytes 1000000 | tf_op jit(solution)/shard_map/pallas_call | solution.py:343
  101.8 1.6 %collective-permute-done.28.theirs = bf16[4,32,1280]{2,1,0:T(8,128)(2,1)S(1)} collective-permute-done((bf16[4,32,1280]{2,1,0:T(8,128)(2,1)S(1)}, bf16[4,32,1280]{2,1,0:T(8,128)(2,1)S(1)}, u32[]{:S(2)}, u32[]{:S(2)}) %collective-permute-start.28) | collective-permute-done | bytes 327712 | tf_op jit(solution)/shard_map/ppermute | solution.py:16
  103.5 3.2 %collective-permute-start.30 = (bf16[32,2048]{1,0:T(8,128)(2,1)S(1)}, bf16[32,2048]{1,0:T(8,128)(2,1)S(1)}, u32[]{:S(2)}, u32[]{:S(2)}) collective-permute-start(bf16[32,2048]{1,0:T(8,128)(2,1)S(1)} %get-tuple-element.82), channel_id=1, source_target_pairs={{0,96},{16,112},{32,0},{48,16},{64,32},{80,48},{96,64},{112,80},{1... | collective-permute-start | bytes 393224 | tf_op jit(solution)/shard_map/ppermute | solution.py:21
  106.8 3.5 %collective-permute-done.29.a = bf16[32,2048]{1,0:T(8,128)(2,1)S(1)} collective-permute-done((bf16[32,2048]{1,0:T(8,128)(2,1)S(1)}, bf16[32,2048]{1,0:T(8,128)(2,1)S(1)}, u32[]{:S(2)}, u32[]{:S(2)}) %collective-permute-start.29) | collective-permute-done | bytes 131104 | tf_op jit(solution)/shard_map/ppermute | solution.py:21
  110.3 2.1 %collective-permute-done.30.b = bf16[32,2048]{1,0:T(8,128)(2,1)S(1)} collective-permute-done((bf16[32,2048]{1,0:T(8,128)(2,1)S(1)}, bf16[32,2048]{1,0:T(8,128)(2,1)S(1)}, u32[]{:S(2)}, u32[]{:S(2)}) %collective-permute-start.30) | collective-permute-done | bytes 131104 | tf_op jit(solution)/shard_map/ppermute | solution.py:21
  113.4 1.5 %shard_map.142 = (f32[2,64,1920]{2,1,0:T(8,128)}, f32[64,1920]{1,0:T(8,128)}) custom-call(bf16[64,2944]{1,0:T(8,128)(2,1)S(1)} %shard_map.136.a.refs_0_, bf16[64,2944]{1,0:T(8,128)(2,1)S(1)} %collective-permute-done.25.b.refs_1_, bf16[64,2944]{1,0:T(8,128)(2,1)S(1)} %collective-permute-done.26.c.refs_2_, ...), custom_call_target="tpu_custom_call" | custom-call | flops 4000000000 | bytes 1000000 | tf_op jit(solution)/shard_map/pallas_call | solution.py:273
  (82 shorter events, 32.7 us)
Async XLA Ops:
  2.2 6.5 %collective-permute-start = (bf16[32,1024]{1,0:T(8,128)(2,1)S(1)}, bf16[32,1024]{1,0:T(8,128)(2,1)S(1)}, u32[]{:S(2)}, u32[]{:S(2)}) collective-permute-start(bf16[32,1024]{1,0:T(8,128)(2,1)S(1)} %shard_map.127), channel_id=1, source_target_pairs={{0,16},{16,0},{32,48},{48,32},{64,80},{80,64},{96,112},{112,96},{1... | collective-permute-start | bytes 196616 | tf_op jit(solution)/shard_map/ppermute | solution.py:16
  8.7 6.3 %collective-permute-start.1 = (bf16[64,1024]{1,0:T(8,128)(2,1)S(1)}, bf16[64,1024]{1,0:T(8,128)(2,1)S(1)}, u32[]{:S(2)}, u32[]{:S(2)}) collective-permute-start(bf16[64,1024]{1,0:T(8,128)(2,1)S(1)} %pad_maximum_fusion), channel_id=1, source_target_pairs={{0,96},{16,112},{32,0},{48,16},{64,32},{80,48},{96,64},{112,80},{1... | collective-permute-start | bytes 393224 | tf_op jit(solution)/shard_map/ppermute | solution.py:21
  11.7 9.6 %collective-permute-start.3 = (bf16[64,1024]{1,0:T(8,128)(2,1)S(1)}, bf16[64,1024]{1,0:T(8,128)(2,1)S(1)}, u32[]{:S(2)}, u32[]{:S(2)}) collective-permute-start(bf16[64,1024]{1,0:T(8,128)(2,1)S(1)} %pad_maximum_fusion), channel_id=1, source_target_pairs={{0,32},{16,48},{32,64},{48,80},{64,96},{80,112},{96,0},{112,16},{1... | collective-permute-start | bytes 393224 | tf_op jit(solution)/shard_map/ppermute | solution.py:21
  11.7 8.8 %collective-permute-start.2 = (bf16[64,1024]{1,0:T(8,128)(2,1)S(1)}, bf16[64,1024]{1,0:T(8,128)(2,1)S(1)}, u32[]{:S(2)}, u32[]{:S(2)}) collective-permute-start(bf16[64,1024]{1,0:T(8,128)(2,1)S(1)} %pad_maximum_fusion), channel_id=1, source_target_pairs={{0,64},{16,80},{32,96},{48,112},{64,0},{80,16},{96,32},{112,48},{1... | collective-permute-start | bytes 393224 | tf_op jit(solution)/shard_map/ppermute | solution.py:21
  22.8 8.9 %collective-permute-start.10 = (bf16[64,2944]{1,0:T(8,128)(2,1)S(1)}, bf16[64,2944]{1,0:T(8,128)(2,1)S(1)}, u32[]{:S(2)}, u32[]{:S(2)}) collective-permute-start(bf16[64,2944]{1,0:T(8,128)(2,1)S(1)} %get-tuple-element.67), channel_id=1, source_target_pairs={{0,4},{1,5},{2,6},{3,7},{4,8},{5,9},{6,10},{7,11},{8,12},{9,13},{1... | collective-permute-start | bytes 1130504 | tf_op jit(solution)/shard_map/ppermute | solution.py:38
  24.5 7.6 %collective-permute-start.11 = (bf16[64,2944]{1,0:T(8,128)(2,1)S(1)}, bf16[64,2944]{1,0:T(8,128)(2,1)S(1)}, u32[]{:S(2)}, u32[]{:S(2)}) collective-permute-start(bf16[64,2944]{1,0:T(8,128)(2,1)S(1)} %get-tuple-element.68), channel_id=1, source_target_pairs={{0,12},{1,13},{2,14},{3,15},{4,0},{5,1},{6,2},{7,3},{8,4},{9,5},{1... | collective-permute-start | bytes 1130504 | tf_op jit(solution)/shard_map/ppermute | solution.py:38
  26.1 10.9 %collective-permute-start.12 = (bf16[64,2944]{1,0:T(8,128)(2,1)S(1)}, bf16[64,2944]{1,0:T(8,128)(2,1)S(1)}, u32[]{:S(2)}, u32[]{:S(2)}) collective-permute-start(bf16[64,2944]{1,0:T(8,128)(2,1)S(1)} %get-tuple-element.69), channel_id=1, source_target_pairs={{0,8},{1,9},{2,10},{3,11},{4,12},{5,13},{6,14},{7,15},{8,0},{9,1},... | collective-permute-start | bytes 1130504 | tf_op jit(solution)/shard_map/ppermute | solution.py:38
  37.1 9.0 %collective-permute-start.13 = (bf16[16,2944]{1,0:T(8,128)(2,1)S(1)}, bf16[16,2944]{1,0:T(8,128)(2,1)S(1)}, u32[]{:S(2)}, u32[]{:S(2)}) collective-permute-start(bf16[16,2944]{1,0:T(8,128)(2,1)S(1)} %get-tuple-element.71), channel_id=1, source_target_pairs={{0,1},{1,2},{2,3},{3,0},{4,5},{5,6},{6,7},{7,4},{8,9},{9,10},{10,1... | collective-permute-start | bytes 282632 | tf_op jit(solution)/shard_map/ppermute | solution.py:38
  40.3 25.0 %collective-permute-start.4 = (bf16[64,3072]{1,0:T(8,128)(2,1)S(1)}, bf16[64,3072]{1,0:T(8,128)(2,1)S(1)}, u32[]{:S(2)}, u32[]{:S(2)}) collective-permute-start(bf16[64,3072]{1,0:T(8,128)(2,1)S(1)} %get-tuple-element.59), channel_id=1, source_target_pairs={{0,4},{1,5},{2,6},{3,7},{4,8},{5,9},{6,10},{7,11},{8,12},{9,13},{1... | collective-permute-start | bytes 1179656 | tf_op jit(solution)/shard_map/ppermute | solution.py:38
  41.8 23.5 %collective-permute-start.5 = (bf16[64,3072]{1,0:T(8,128)(2,1)S(1)}, bf16[64,3072]{1,0:T(8,128)(2,1)S(1)}, u32[]{:S(2)}, u32[]{:S(2)}) collective-permute-start(bf16[64,3072]{1,0:T(8,128)(2,1)S(1)} %get-tuple-element.60), channel_id=1, source_target_pairs={{0,12},{1,13},{2,14},{3,15},{4,0},{5,1},{6,2},{7,3},{8,4},{9,5},{1... | collective-permute-start | bytes 1179656 | tf_op jit(solution)/shard_map/ppermute | solution.py:38
  43.6 21.7 %collective-permute-start.6 = (bf16[64,3072]{1,0:T(8,128)(2,1)S(1)}, bf16[64,3072]{1,0:T(8,128)(2,1)S(1)}, u32[]{:S(2)}, u32[]{:S(2)}) collective-permute-start(bf16[64,3072]{1,0:T(8,128)(2,1)S(1)} %get-tuple-element.61), channel_id=1, source_target_pairs={{0,8},{1,9},{2,10},{3,11},{4,12},{5,13},{6,14},{7,15},{8,0},{9,1},... | collective-permute-start | bytes 1179656 | tf_op jit(solution)/shard_map/ppermute | solution.py:38
  44.0 8.6 %collective-permute-start.14 = (bf16[16,2944]{1,0:T(8,128)(2,1)S(1)}, bf16[16,2944]{1,0:T(8,128)(2,1)S(1)}, u32[]{:S(2)}, u32[]{:S(2)}) collective-permute-start(bf16[16,2944]{1,0:T(8,128)(2,1)S(1)} %get-tuple-element.72), channel_id=1, source_target_pairs={{0,3},{1,0},{2,1},{3,2},{4,7},{5,4},{6,5},{7,6},{8,11},{9,8},{10,9... | collective-permute-start | bytes 282632 | tf_op jit(solution)/shard_map/ppermute | solution.py:38
  46.1 7.1 %collective-permute-start.15 = (bf16[16,2944]{1,0:T(8,128)(2,1)S(1)}, bf16[16,2944]{1,0:T(8,128)(2,1)S(1)}, u32[]{:S(2)}, u32[]{:S(2)}) collective-permute-start(bf16[16,2944]{1,0:T(8,128)(2,1)S(1)} %get-tuple-element.73), channel_id=1, source_target_pairs={{0,2},{1,3},{2,0},{3,1},{4,6},{5,7},{6,4},{7,5},{8,10},{9,11},{10,... | collective-permute-start | bytes 282632 | tf_op jit(solution)/shard_map/ppermute | solution.py:38
  53.4 5.9 %collective-permute-start.24 = (bf16[16,2944]{1,0:T(8,128)(2,1)S(1)}, bf16[16,2944]{1,0:T(8,128)(2,1)S(1)}, u32[]{:S(2)}, u32[]{:S(2)}) collective-permute-start(bf16[16,2944]{1,0:T(8,128)(2,1)S(1)} %shard_map.133.first.a), channel_id=1, source_target_pairs={{0,1},{1,2},{2,3},{3,0},{4,5},{5,6},{6,7},{7,4},{8,9},{9,10},{10,1... | collective-permute-start | bytes 282632 | tf_op jit(solution)/shard_map/ppermute | solution.py:38
  54.9 6.7 %collective-permute-start.23 = (bf16[16,2944]{1,0:T(8,128)(2,1)S(1)}, bf16[16,2944]{1,0:T(8,128)(2,1)S(1)}, u32[]{:S(2)}, u32[]{:S(2)}) collective-permute-start(bf16[16,2944]{1,0:T(8,128)(2,1)S(1)} %shard_map.133.first.a), channel_id=1, source_target_pairs={{0,2},{1,3},{2,0},{3,1},{4,6},{5,7},{6,4},{7,5},{8,10},{9,11},{10,... | collective-permute-start | bytes 282632 | tf_op jit(solution)/shard_map/ppermute | solution.py:38
  59.3 4.6 %collective-permute-start.22 = (bf16[16,2944]{1,0:T(8,128)(2,1)S(1)}, bf16[16,2944]{1,0:T(8,128)(2,1)S(1)}, u32[]{:S(2)}, u32[]{:S(2)}) collective-permute-start(bf16[16,2944]{1,0:T(8,128)(2,1)S(1)} %shard_map.133.first.a), channel_id=1, source_target_pairs={{0,3},{1,0},{2,1},{3,2},{4,7},{5,4},{6,5},{7,6},{8,11},{9,8},{10,9... | collective-permute-start | bytes 282632 | tf_op jit(solution)/shard_map/ppermute | solution.py:38
  63.9 24.7 %collective-permute-start.27 = (bf16[64,2944]{1,0:T(8,128)(2,1)S(1)}, bf16[64,2944]{1,0:T(8,128)(2,1)S(1)}, u32[]{:S(2)}, u32[]{:S(2)}) collective-permute-start(bf16[64,2944]{1,0:T(8,128)(2,1)S(1)} %shard_map.136.a.refs_0_), channel_id=1, source_target_pairs={{0,4},{1,5},{2,6},{3,7},{4,8},{5,9},{6,10},{7,11},{8,12},{9,13},{1... | collective-permute-start | bytes 1130504 | tf_op jit(solution)/shard_map/ppermute | solution.py:38
  65.5 5.9 %collective-permute-start.7 = (bf16[16,3072]{1,0:T(8,128)(2,1)S(1)}, bf16[16,3072]{1,0:T(8,128)(2,1)S(1)}, u32[]{:S(2)}, u32[]{:S(2)}) collective-permute-start(bf16[16,3072]{1,0:T(8,128)(2,1)S(1)} %get-tuple-element.63), channel_id=1, source_target_pairs={{0,1},{1,2},{2,3},{3,0},{4,5},{5,6},{6,7},{7,4},{8,9},{9,10},{10,1... | collective-permute-start | bytes 294920 | tf_op jit(solution)/shard_map/ppermute | solution.py:38
  65.7 5.7 %collective-permute-start.8 = (bf16[16,3072]{1,0:T(8,128)(2,1)S(1)}, bf16[16,3072]{1,0:T(8,128)(2,1)S(1)}, u32[]{:S(2)}, u32[]{:S(2)}) collective-permute-start(bf16[16,3072]{1,0:T(8,128)(2,1)S(1)} %get-tuple-element.64), channel_id=1, source_target_pairs={{0,3},{1,0},{2,1},{3,2},{4,7},{5,4},{6,5},{7,6},{8,11},{9,8},{10,9... | collective-permute-start | bytes 294920 | tf_op jit(solution)/shard_map/ppermute | solution.py:38
  68.9 6.1 %collective-permute-start.9 = (bf16[16,3072]{1,0:T(8,128)(2,1)S(1)}, bf16[16,3072]{1,0:T(8,128)(2,1)S(1)}, u32[]{:S(2)}, u32[]{:S(2)}) collective-permute-start(bf16[16,3072]{1,0:T(8,128)(2,1)S(1)} %get-tuple-element.65), channel_id=1, source_target_pairs={{0,2},{1,3},{2,0},{3,1},{4,6},{5,7},{6,4},{7,5},{8,10},{9,11},{10,... | collective-permute-start | bytes 294920 | tf_op jit(solution)/shard_map/ppermute | solution.py:38
  75.3 7.3 %collective-permute-start.18 = (bf16[16,3072]{1,0:T(8,128)(2,1)S(1)}, bf16[16,3072]{1,0:T(8,128)(2,1)S(1)}, u32[]{:S(2)}, u32[]{:S(2)}) collective-permute-start(bf16[16,3072]{1,0:T(8,128)(2,1)S(1)} %shard_map.134.a), channel_id=1, source_target_pairs={{0,1},{1,2},{2,3},{3,0},{4,5},{5,6},{6,7},{7,4},{8,9},{9,10},{10,1... | collective-permute-start | bytes 294920 | tf_op jit(solution)/shard_map/ppermute | solution.py:38
  75.7 8.8 %collective-permute-start.17 = (bf16[16,3072]{1,0:T(8,128)(2,1)S(1)}, bf16[16,3072]{1,0:T(8,128)(2,1)S(1)}, u32[]{:S(2)}, u32[]{:S(2)}) collective-permute-start(bf16[16,3072]{1,0:T(8,128)(2,1)S(1)} %shard_map.134.a), channel_id=1, source_target_pairs={{0,2},{1,3},{2,0},{3,1},{4,6},{5,7},{6,4},{7,5},{8,10},{9,11},{10,... | collective-permute-start | bytes 294920 | tf_op jit(solution)/shard_map/ppermute | solution.py:38
  78.8 6.4 %collective-permute-start.16 = (bf16[16,3072]{1,0:T(8,128)(2,1)S(1)}, bf16[16,3072]{1,0:T(8,128)(2,1)S(1)}, u32[]{:S(2)}, u32[]{:S(2)}) collective-permute-start(bf16[16,3072]{1,0:T(8,128)(2,1)S(1)} %shard_map.134.a), channel_id=1, source_target_pairs={{0,3},{1,0},{2,1},{3,2},{4,7},{5,4},{6,5},{7,6},{8,11},{9,8},{10,9... | collective-permute-start | bytes 294920 | tf_op jit(solution)/shard_map/ppermute | solution.py:38
  79.4 10.8 %collective-permute-start.26 = (bf16[64,2944]{1,0:T(8,128)(2,1)S(1)}, bf16[64,2944]{1,0:T(8,128)(2,1)S(1)}, u32[]{:S(2)}, u32[]{:S(2)}) collective-permute-start(bf16[64,2944]{1,0:T(8,128)(2,1)S(1)} %shard_map.136.a.refs_0_), channel_id=1, source_target_pairs={{0,8},{1,9},{2,10},{3,11},{4,12},{5,13},{6,14},{7,15},{8,0},{9,1},... | collective-permute-start | bytes 1130504 | tf_op jit(solution)/shard_map/ppermute | solution.py:38
  82.6 8.9 %collective-permute-start.25 = (bf16[64,2944]{1,0:T(8,128)(2,1)S(1)}, bf16[64,2944]{1,0:T(8,128)(2,1)S(1)}, u32[]{:S(2)}, u32[]{:S(2)}) collective-permute-start(bf16[64,2944]{1,0:T(8,128)(2,1)S(1)} %shard_map.136.a.refs_0_), channel_id=1, source_target_pairs={{0,12},{1,13},{2,14},{3,15},{4,0},{5,1},{6,2},{7,3},{8,4},{9,5},{1... | collective-permute-start | bytes 1130504 | tf_op jit(solution)/shard_map/ppermute | solution.py:38
  85.2 9.1 %collective-permute-start.21 = (bf16[64,3072]{1,0:T(8,128)(2,1)S(1)}, bf16[64,3072]{1,0:T(8,128)(2,1)S(1)}, u32[]{:S(2)}, u32[]{:S(2)}) collective-permute-start(bf16[64,3072]{1,0:T(8,128)(2,1)S(1)} %shard_map.135.a.refs_4_), channel_id=1, source_target_pairs={{0,4},{1,5},{2,6},{3,7},{4,8},{5,9},{6,10},{7,11},{8,12},{9,13},{1... | collective-permute-start | bytes 1179656 | tf_op jit(solution)/shard_map/ppermute | solution.py:38
  86.6 12.0 %collective-permute-start.20 = (bf16[64,3072]{1,0:T(8,128)(2,1)S(1)}, bf16[64,3072]{1,0:T(8,128)(2,1)S(1)}, u32[]{:S(2)}, u32[]{:S(2)}) collective-permute-start(bf16[64,3072]{1,0:T(8,128)(2,1)S(1)} %shard_map.135.a.refs_4_), channel_id=1, source_target_pairs={{0,8},{1,9},{2,10},{3,11},{4,12},{5,13},{6,14},{7,15},{8,0},{9,1},... | collective-permute-start | bytes 1179656 | tf_op jit(solution)/shard_map/ppermute | solution.py:38
  88.6 11.4 %collective-permute-start.19 = (bf16[64,3072]{1,0:T(8,128)(2,1)S(1)}, bf16[64,3072]{1,0:T(8,128)(2,1)S(1)}, u32[]{:S(2)}, u32[]{:S(2)}) collective-permute-start(bf16[64,3072]{1,0:T(8,128)(2,1)S(1)} %shard_map.135.a.refs_4_), channel_id=1, source_target_pairs={{0,12},{1,13},{2,14},{3,15},{4,0},{5,1},{6,2},{7,3},{8,4},{9,5},{1... | collective-permute-start | bytes 1179656 | tf_op jit(solution)/shard_map/ppermute | solution.py:38
  101.7 1.7 %collective-permute-start.28 = (bf16[4,32,1280]{2,1,0:T(8,128)(2,1)S(1)}, bf16[4,32,1280]{2,1,0:T(8,128)(2,1)S(1)}, u32[]{:S(2)}, u32[]{:S(2)}) collective-permute-start(bf16[4,32,1280]{2,1,0:T(8,128)(2,1)S(1)} %get-tuple-element.78), channel_id=1, source_target_pairs={{0,16},{16,0},{32,48},{48,32},{64,80},{80,64},{96,112},{112,96},{1... | collective-permute-start | bytes 983048 | tf_op jit(solution)/shard_map/ppermute | solution.py:16
  103.5 6.8 %collective-permute-start.29 = (bf16[32,2048]{1,0:T(8,128)(2,1)S(1)}, bf16[32,2048]{1,0:T(8,128)(2,1)S(1)}, u32[]{:S(2)}, u32[]{:S(2)}) collective-permute-start(bf16[32,2048]{1,0:T(8,128)(2,1)S(1)} %get-tuple-element.81), channel_id=1, source_target_pairs={{0,32},{16,48},{32,64},{48,80},{64,96},{80,112},{96,0},{112,16},{1... | collective-permute-start | bytes 393224 | tf_op jit(solution)/shard_map/ppermute | solution.py:21
  103.5 8.8 %collective-permute-start.30 = (bf16[32,2048]{1,0:T(8,128)(2,1)S(1)}, bf16[32,2048]{1,0:T(8,128)(2,1)S(1)}, u32[]{:S(2)}, u32[]{:S(2)}) collective-permute-start(bf16[32,2048]{1,0:T(8,128)(2,1)S(1)} %get-tuple-element.82), channel_id=1, source_target_pairs={{0,96},{16,112},{32,0},{48,16},{64,32},{80,48},{96,64},{112,80},{1... | collective-permute-start | bytes 393224 | tf_op jit(solution)/shard_map/ppermute | solution.py:21
  106.8 6.5 %collective-permute-start.31 = (bf16[32,2048]{1,0:T(8,128)(2,1)S(1)}, bf16[32,2048]{1,0:T(8,128)(2,1)S(1)}, u32[]{:S(2)}, u32[]{:S(2)}) collective-permute-start(bf16[32,2048]{1,0:T(8,128)(2,1)S(1)} %get-tuple-element.83), channel_id=1, source_target_pairs={{0,64},{16,80},{32,96},{48,112},{64,0},{80,16},{96,32},{112,48},{1... | collective-permute-start | bytes 393224 | tf_op jit(solution)/shard_map/ppermute | solution.py:21
  (13 other events, 159.8 us)
where the time goes:
time: 118 us; the launch traced here: 116 us
  waiting for transfers between devices  49.5 us (42%)
  starting transfers between devices  48.3 us (41%)
  Pallas kernels  10.1 us (9%)
  local copies, waits for them, and re-layouts  6.98 us (6%)
    ppermute x24, starting transfers between devices, along(): return lax.ppermute(x, ('dp', 'y', 'z'), pairs)  39.5 us
    ppermute x24, waiting for transfers between devices, along(): return lax.ppermute(x, ('dp', 'y', 'z'), pairs)  34.1 us
    ppermute x6, waiting for transfers between devices, to_chip(): return lax.ppermute(x, 'dp', [(i, (i + 2 * by) % n) for i in range(n)])  13.8 us
    ppermute x6, starting transfers between devices, to_chip(): return lax.ppermute(x, 'dp', [(i, (i + 2 * by) % n) for i in range(n)])  8.53 us
    unnamed x28, local copies, waits for them, and re-layouts  6.97 us
  transfers between devices with their start and end apart: 33, of which 24 were waited for; matrix products, arithmetic and copies ran while one was open for 0% of the time, Pallas kernels for 5%

commit v1 on v0

--- a/solution.py
+++ b/solution.py
@@ -354,16 +354,16 @@
     value = [mine[k] + theirs[k].astype(F32) for k in range(4)]
     own[:, :1024] = value[0][:, 256:]
     for j in range(4):
-        own[:, 1024 + 256 * j : 1280 + 256 * j] = value[j][:, :256]
+        own[:, 1024 + 192 * j : 1216 + 192 * j] = value[j][:, :192]
     value = [v.astype(BF16) for v in value]
     for k, out in ((1, one), (2, two), (3, three)):
         out[:, :1024] = value[k][:, 256:]
         for j in range(4):
-            out[:, 1024 + 256 * j : 1280 + 256 * j] = value[(j + k) % 4][:, :256]
+            out[:, 1024 + 192 * j : 1216 + 192 * j] = value[(j + k) % 4][:, :192]
 
 
 def core_sums(mine, theirs):
-    shape = (32, 2048)
+    shape = (32, 1792)
     return pl.pallas_call(
         core_sum_kernel,
         out_shape=[in_vmem(shape, F32)] + [in_vmem(shape, BF16)] * 3,
@@ -380,13 +380,13 @@
     )
     large[...] = value[:, :1024]
     for j in range(4):
-        small[j] = value[:, 1024 + 256 * j : 1280 + 256 * j].astype(BF16)
+        small[j] = value[:, 1024 + 192 * j : 1216 + 192 * j].astype(BF16)
 
 
 def chip_sums(own, got):
     return pl.pallas_call(
         chip_sum_kernel,
-        out_shape=[in_vmem((4, 32, 256), BF16), in_vmem((32, 1024), F32)],
+        out_shape=[in_vmem((4, 32, 192), BF16), in_vmem((32, 1024), F32)],
         in_specs=whole(4),
         out_specs=whole(2),
         compiler_params=params(),

time: 118 us -> 118 us (level)
  no operation moved by 1% of the time
where the time goes in v1:
time: 118 us; the launch traced here: 116 us
  waiting for transfers between devices  49.3 us (42%)
  starting transfers between devices  48.3 us (41%)
  Pallas kernels  10.3 us (9%)
  local copies, waits for them, and re-layouts  6.98 us (6%)
    ppermute x24, starting transfers between devices, along(): return lax.ppermute(x, ('dp', 'y', 'z'), pairs)  39.5 us
    ppermute x24, waiting for transfers between devices, along(): return lax.ppermute(x, ('dp', 'y', 'z'), pairs)  34.1 us
    ppermute x6, waiting for transfers between devices, to_chip(): return lax.ppermute(x, 'dp', [(i, (i + 2 * by) % n) for i in range(n)])  13.6 us
    ppermute x6, starting transfers between devices, to_chip(): return lax.ppermute(x, 'dp', [(i, (i + 2 * by) % n) for i in range(n)])  8.53 us
    unnamed x28, local copies, waits for them, and re-layouts  6.97 us
  transfers between devices with their start and end apart: 33, of which 24 were waited for; matrix products, arithmetic and copies ran while one was open for 0% of the time, Pallas kernels for 5%

profile of v1, /device:TPU:0, one launch (start us, length us, event | category | flops | bytes accessed | tf_op | source)
XLA Modules:
  0.0 115.9 jit_solution(11512086412275442481)
XLA Ops:
  2.4 2.1 %copy-done = bf16[2,512,1920]{2,1,0:T(8,128)(2,1)S(1)} copy-done((bf16[2,512,1920]{2,1,0:T(8,128)(2,1)S(1)}, bf16[2,512,1920]{2,1,0:T(8,128)(2,1)}, u32[]{:S(2)}) %copy-start) | copy-done | bytes 3932184
  4.6 1.5 %copy-done.2 = bf16[1920,512]{1,0:T(8,128)(2,1)S(1)} copy-done((bf16[1920,512]{1,0:T(8,128)(2,1)S(1)}, bf16[1920,512]{1,0:T(8,128)(2,1)}, u32[]{:S(2)}) %copy-start.2) | copy-done | bytes 1966104
  8.7 2.9 %collective-permute-start.1 = (bf16[64,1024]{1,0:T(8,128)(2,1)S(1)}, bf16[64,1024]{1,0:T(8,128)(2,1)S(1)}, u32[]{:S(2)}, u32[]{:S(2)}) collective-permute-start(bf16[64,1024]{1,0:T(8,128)(2,1)S(1)} %pad_maximum_fusion), channel_id=1, source_target_pairs={{0,96},{16,112},{32,0},{48,16},{64,32},{80,48},{96,64},{112,80},{1... | collective-permute-start | bytes 393224 | tf_op jit(solution)/shard_map/ppermute | solution.py:21
  11.7 2.3 %collective-permute-start.2 = (bf16[64,1024]{1,0:T(8,128)(2,1)S(1)}, bf16[64,1024]{1,0:T(8,128)(2,1)S(1)}, u32[]{:S(2)}, u32[]{:S(2)}) collective-permute-start(bf16[64,1024]{1,0:T(8,128)(2,1)S(1)} %pad_maximum_fusion), channel_id=1, source_target_pairs={{0,64},{16,80},{32,96},{48,112},{64,0},{80,16},{96,32},{112,48},{1... | collective-permute-start | bytes 393224 | tf_op jit(solution)/shard_map/ppermute | solution.py:21
  15.1 5.4 %collective-permute-done.2 = bf16[64,1024]{1,0:T(8,128)(2,1)S(1)} collective-permute-done((bf16[64,1024]{1,0:T(8,128)(2,1)S(1)}, bf16[64,1024]{1,0:T(8,128)(2,1)S(1)}, u32[]{:S(2)}, u32[]{:S(2)}) %collective-permute-start.2) | collective-permute-done | bytes 131104 | tf_op jit(solution)/shard_map/ppermute | solution.py:21
  21.3 1.5 %shard_map.129 = (bf16[256,1024]{1,0:T(8,128)(2,1)S(1)}, f32[64,2944]{1,0:T(8,128)S(1)}, bf16[64,2944]{1,0:T(8,128)(2,1)S(1)}, bf16[64,2944]{1,0:T(8,128)(2,1)S(1)}, bf16[64,2944]{1,0:T(8,128)(2,1)S(1)}) custom-call(bf16[256,256]{1,0:T(8,128)(2,1)S(1)} %compare_convert_fusion.turn, bf16[256,1024]{1,0:T(8,128)(2,1)S(1)} %constant_dynamic-update-slice_fusion.near, ...), custom_call_target="tpu_custom_call" | custom-call | flops 1000000000 | bytes 1000000 | tf_op jit(solution)/shard_map/pallas_call | solution.py:134
  22.8 1.6 %collective-permute-start.10 = (bf16[64,2944]{1,0:T(8,128)(2,1)S(1)}, bf16[64,2944]{1,0:T(8,128)(2,1)S(1)}, u32[]{:S(2)}, u32[]{:S(2)}) collective-permute-start(bf16[64,2944]{1,0:T(8,128)(2,1)S(1)} %get-tuple-element.67), channel_id=1, source_target_pairs={{0,4},{1,5},{2,6},{3,7},{4,8},{5,9},{6,10},{7,11},{8,12},{9,13},{1... | collective-permute-start | bytes 1130504 | tf_op jit(solution)/shard_map/ppermute | solution.py:38
  24.5 1.7 %collective-permute-start.11 = (bf16[64,2944]{1,0:T(8,128)(2,1)S(1)}, bf16[64,2944]{1,0:T(8,128)(2,1)S(1)}, u32[]{:S(2)}, u32[]{:S(2)}) collective-permute-start(bf16[64,2944]{1,0:T(8,128)(2,1)S(1)} %get-tuple-element.68), channel_id=1, source_target_pairs={{0,12},{1,13},{2,14},{3,15},{4,0},{5,1},{6,2},{7,3},{8,4},{9,5},{1... | collective-permute-start | bytes 1130504 | tf_op jit(solution)/shard_map/ppermute | solution.py:38
  26.1 2.0 %collective-permute-start.12 = (bf16[64,2944]{1,0:T(8,128)(2,1)S(1)}, bf16[64,2944]{1,0:T(8,128)(2,1)S(1)}, u32[]{:S(2)}, u32[]{:S(2)}) collective-permute-start(bf16[64,2944]{1,0:T(8,128)(2,1)S(1)} %get-tuple-element.69), channel_id=1, source_target_pairs={{0,8},{1,9},{2,10},{3,11},{4,12},{5,13},{6,14},{7,15},{8,0},{9,1},... | collective-permute-start | bytes 1130504 | tf_op jit(solution)/shard_map/ppermute | solution.py:38
  28.1 3.6 %collective-permute-done.10.refs_1_ = bf16[64,2944]{1,0:T(8,128)(2,1)S(1)} collective-permute-done((bf16[64,2944]{1,0:T(8,128)(2,1)S(1)}, bf16[64,2944]{1,0:T(8,128)(2,1)S(1)}, u32[]{:S(2)}, u32[]{:S(2)}) %collective-permute-start.10) | collective-permute-done | bytes 376864 | tf_op jit(solution)/shard_map/ppermute | solution.py:38
  32.1 4.9 %collective-permute-done.12.refs_3_ = bf16[64,2944]{1,0:T(8,128)(2,1)S(1)} collective-permute-done((bf16[64,2944]{1,0:T(8,128)(2,1)S(1)}, bf16[64,2944]{1,0:T(8,128)(2,1)S(1)}, u32[]{:S(2)}, u32[]{:S(2)}) %collective-permute-start.12) | collective-permute-done | bytes 376864 | tf_op jit(solution)/shard_map/ppermute | solution.py:38
  37.1 2.0 %collective-permute-start.13 = (bf16[16,2944]{1,0:T(8,128)(2,1)S(1)}, bf16[16,2944]{1,0:T(8,128)(2,1)S(1)}, u32[]{:S(2)}, u32[]{:S(2)}) collective-permute-start(bf16[16,2944]{1,0:T(8,128)(2,1)S(1)} %get-tuple-element.71), channel_id=1, source_target_pairs={{0,1},{1,2},{2,3},{3,0},{4,5},{5,6},{6,7},{7,4},{8,9},{9,10},{10,1... | collective-permute-start | bytes 282632 | tf_op jit(solution)/shard_map/ppermute | solution.py:38
  41.8 1.8 %collective-permute-start.5 = (bf16[64,3072]{1,0:T(8,128)(2,1)S(1)}, bf16[64,3072]{1,0:T(8,128)(2,1)S(1)}, u32[]{:S(2)}, u32[]{:S(2)}) collective-permute-start(bf16[64,3072]{1,0:T(8,128)(2,1)S(1)} %get-tuple-element.60), channel_id=1, source_target_pairs={{0,12},{1,13},{2,14},{3,15},{4,0},{5,1},{6,2},{7,3},{8,4},{9,5},{1... | collective-permute-start | bytes 1179656 | tf_op jit(solution)/shard_map/ppermute | solution.py:38
  44.0 2.1 %collective-permute-start.14 = (bf16[16,2944]{1,0:T(8,128)(2,1)S(1)}, bf16[16,2944]{1,0:T(8,128)(2,1)S(1)}, u32[]{:S(2)}, u32[]{:S(2)}) collective-permute-start(bf16[16,2944]{1,0:T(8,128)(2,1)S(1)} %get-tuple-element.72), channel_id=1, source_target_pairs={{0,3},{1,0},{2,1},{3,2},{4,7},{5,4},{6,5},{7,6},{8,11},{9,8},{10,9... | collective-permute-start | bytes 282632 | tf_op jit(solution)/shard_map/ppermute | solution.py:38
  46.1 1.9 %collective-permute-start.15 = (bf16[16,2944]{1,0:T(8,128)(2,1)S(1)}, bf16[16,2944]{1,0:T(8,128)(2,1)S(1)}, u32[]{:S(2)}, u32[]{:S(2)}) collective-permute-start(bf16[16,2944]{1,0:T(8,128)(2,1)S(1)} %get-tuple-element.73), channel_id=1, source_target_pairs={{0,2},{1,3},{2,0},{3,1},{4,6},{5,7},{6,4},{7,5},{8,10},{9,11},{10,... | collective-permute-start | bytes 282632 | tf_op jit(solution)/shard_map/ppermute | solution.py:38
  48.0 4.6 %collective-permute-done.14.c = bf16[16,2944]{1,0:T(8,128)(2,1)S(1)} collective-permute-done((bf16[16,2944]{1,0:T(8,128)(2,1)S(1)}, bf16[16,2944]{1,0:T(8,128)(2,1)S(1)}, u32[]{:S(2)}, u32[]{:S(2)}) %collective-permute-start.14) | collective-permute-done | bytes 94240 | tf_op jit(solution)/shard_map/ppermute | solution.py:38
  54.9 3.1 %collective-permute-start.23 = (bf16[16,2944]{1,0:T(8,128)(2,1)S(1)}, bf16[16,2944]{1,0:T(8,128)(2,1)S(1)}, u32[]{:S(2)}, u32[]{:S(2)}) collective-permute-start(bf16[16,2944]{1,0:T(8,128)(2,1)S(1)} %shard_map.133.first.a), channel_id=1, source_target_pairs={{0,2},{1,3},{2,0},{3,1},{4,6},{5,7},{6,4},{7,5},{8,10},{9,11},{10,... | collective-permute-start | bytes 282632 | tf_op jit(solution)/shard_map/ppermute | solution.py:38
  59.3 1.8 %collective-permute-start.22 = (bf16[16,2944]{1,0:T(8,128)(2,1)S(1)}, bf16[16,2944]{1,0:T(8,128)(2,1)S(1)}, u32[]{:S(2)}, u32[]{:S(2)}) collective-permute-start(bf16[16,2944]{1,0:T(8,128)(2,1)S(1)} %shard_map.133.first.a), channel_id=1, source_target_pairs={{0,3},{1,0},{2,1},{3,2},{4,7},{5,4},{6,5},{7,6},{8,11},{9,8},{10,9... | collective-permute-start | bytes 282632 | tf_op jit(solution)/shard_map/ppermute | solution.py:38
  61.5 2.3 %collective-permute-done.22.b = bf16[16,2944]{1,0:T(8,128)(2,1)S(1)} collective-permute-done((bf16[16,2944]{1,0:T(8,128)(2,1)S(1)}, bf16[16,2944]{1,0:T(8,128)(2,1)S(1)}, u32[]{:S(2)}, u32[]{:S(2)}) %collective-permute-start.22) | collective-permute-done | bytes 94240 | tf_op jit(solution)/shard_map/ppermute | solution.py:38
  65.7 3.2 %collective-permute-start.8 = (bf16[16,3072]{1,0:T(8,128)(2,1)S(1)}, bf16[16,3072]{1,0:T(8,128)(2,1)S(1)}, u32[]{:S(2)}, u32[]{:S(2)}) collective-permute-start(bf16[16,3072]{1,0:T(8,128)(2,1)S(1)} %get-tuple-element.64), channel_id=1, source_target_pairs={{0,3},{1,0},{2,1},{3,2},{4,7},{5,4},{6,5},{7,6},{8,11},{9,8},{10,9... | collective-permute-start | bytes 294920 | tf_op jit(solution)/shard_map/ppermute | solution.py:38
  71.4 3.6 %collective-permute-done.9.d = bf16[16,3072]{1,0:T(8,128)(2,1)S(1)} collective-permute-done((bf16[16,3072]{1,0:T(8,128)(2,1)S(1)}, bf16[16,3072]{1,0:T(8,128)(2,1)S(1)}, u32[]{:S(2)}, u32[]{:S(2)}) %collective-permute-start.9) | collective-permute-done | bytes 98336 | tf_op jit(solution)/shard_map/ppermute | solution.py:38
  75.7 3.1 %collective-permute-start.17 = (bf16[16,3072]{1,0:T(8,128)(2,1)S(1)}, bf16[16,3072]{1,0:T(8,128)(2,1)S(1)}, u32[]{:S(2)}, u32[]{:S(2)}) collective-permute-start(bf16[16,3072]{1,0:T(8,128)(2,1)S(1)} %shard_map.134.a), channel_id=1, source_target_pairs={{0,2},{1,3},{2,0},{3,1},{4,6},{5,7},{6,4},{7,5},{8,10},{9,11},{10,... | collective-permute-start | bytes 294920 | tf_op jit(solution)/shard_map/ppermute | solution.py:38
  79.4 1.8 %collective-permute-start.26 = (bf16[64,2944]{1,0:T(8,128)(2,1)S(1)}, bf16[64,2944]{1,0:T(8,128)(2,1)S(1)}, u32[]{:S(2)}, u32[]{:S(2)}) collective-permute-start(bf16[64,2944]{1,0:T(8,128)(2,1)S(1)} %shard_map.136.a.refs_0_), channel_id=1, source_target_pairs={{0,8},{1,9},{2,10},{3,11},{4,12},{5,13},{6,14},{7,15},{8,0},{9,1},... | collective-permute-start | bytes 1130504 | tf_op jit(solution)/shard_map/ppermute | solution.py:38
  86.6 2.0 %collective-permute-start.20 = (bf16[64,3072]{1,0:T(8,128)(2,1)S(1)}, bf16[64,3072]{1,0:T(8,128)(2,1)S(1)}, u32[]{:S(2)}, u32[]{:S(2)}) collective-permute-start(bf16[64,3072]{1,0:T(8,128)(2,1)S(1)} %shard_map.135.a.refs_4_), channel_id=1, source_target_pairs={{0,8},{1,9},{2,10},{3,11},{4,12},{5,13},{6,14},{7,15},{8,0},{9,1},... | collective-permute-start | bytes 1179656 | tf_op jit(solution)/shard_map/ppermute | solution.py:38
  88.6 1.6 %collective-permute-start.19 = (bf16[64,3072]{1,0:T(8,128)(2,1)S(1)}, bf16[64,3072]{1,0:T(8,128)(2,1)S(1)}, u32[]{:S(2)}, u32[]{:S(2)}) collective-permute-start(bf16[64,3072]{1,0:T(8,128)(2,1)S(1)} %shard_map.135.a.refs_4_), channel_id=1, source_target_pairs={{0,12},{1,13},{2,14},{3,15},{4,0},{5,1},{6,2},{7,3},{8,4},{9,5},{1... | collective-permute-start | bytes 1179656 | tf_op jit(solution)/shard_map/ppermute | solution.py:38
  94.3 4.3 %collective-permute-done.20.c.refs_6_ = bf16[64,3072]{1,0:T(8,128)(2,1)S(1)} collective-permute-done((bf16[64,3072]{1,0:T(8,128)(2,1)S(1)}, bf16[64,3072]{1,0:T(8,128)(2,1)S(1)}, u32[]{:S(2)}, u32[]{:S(2)}) %collective-permute-start.20) | collective-permute-done | bytes 393248 | tf_op jit(solution)/shard_map/ppermute | solution.py:38
  100.0 1.7 %shard_map.138 = (f32[4,32,1280]{2,1,0:T(8,128)S(1)}, bf16[4,32,1280]{2,1,0:T(8,128)(2,1)S(1)}) custom-call(bf16[64,3072]{1,0:T(8,128)(2,1)S(1)} %shard_map.135.a.refs_4_, bf16[64,3072]{1,0:T(8,128)(2,1)S(1)} %collective-permute-done.19.b.refs_5_, bf16[64,3072]{1,0:T(8,128)(2,1)S(1)} %collective-permute-done.20.c.refs_6_, ...), custom_call_target="tpu_custom_call" | custom-call | flops 1000000000 | bytes 1000000 | tf_op jit(solution)/shard_map/pallas_call | solution.py:343
  101.8 1.6 %collective-permute-done.28.theirs = bf16[4,32,1280]{2,1,0:T(8,128)(2,1)S(1)} collective-permute-done((bf16[4,32,1280]{2,1,0:T(8,128)(2,1)S(1)}, bf16[4,32,1280]{2,1,0:T(8,128)(2,1)S(1)}, u32[]{:S(2)}, u32[]{:S(2)}) %collective-permute-start.28) | collective-permute-done | bytes 327712 | tf_op jit(solution)/shard_map/ppermute | solution.py:16
  103.6 3.2 %collective-permute-start.30 = (bf16[32,1792]{1,0:T(8,128)(2,1)S(1)}, bf16[32,1792]{1,0:T(8,128)(2,1)S(1)}, u32[]{:S(2)}, u32[]{:S(2)}) collective-permute-start(bf16[32,1792]{1,0:T(8,128)(2,1)S(1)} %get-tuple-element.82), channel_id=1, source_target_pairs={{0,96},{16,112},{32,0},{48,16},{64,32},{80,48},{96,64},{112,80},{1... | collective-permute-start | bytes 344072 | tf_op jit(solution)/shard_map/ppermute | solution.py:21
  106.8 3.2 %collective-permute-done.29.a = bf16[32,1792]{1,0:T(8,128)(2,1)S(1)} collective-permute-done((bf16[32,1792]{1,0:T(8,128)(2,1)S(1)}, bf16[32,1792]{1,0:T(8,128)(2,1)S(1)}, u32[]{:S(2)}, u32[]{:S(2)}) %collective-permute-start.29) | collective-permute-done | bytes 114720 | tf_op jit(solution)/shard_map/ppermute | solution.py:21
  110.0 1.7 %collective-permute-done.30.b = bf16[32,1792]{1,0:T(8,128)(2,1)S(1)} collective-permute-done((bf16[32,1792]{1,0:T(8,128)(2,1)S(1)}, bf16[32,1792]{1,0:T(8,128)(2,1)S(1)}, u32[]{:S(2)}, u32[]{:S(2)}) %collective-permute-start.30) | collective-permute-done | bytes 114720 | tf_op jit(solution)/shard_map/ppermute | solution.py:21
  113.4 1.5 %shard_map.142 = (f32[2,64,1920]{2,1,0:T(8,128)}, f32[64,1920]{1,0:T(8,128)}) custom-call(bf16[64,2944]{1,0:T(8,128)(2,1)S(1)} %shard_map.136.a.refs_0_, bf16[64,2944]{1,0:T(8,128)(2,1)S(1)} %collective-permute-done.25.b.refs_1_, bf16[64,2944]{1,0:T(8,128)(2,1)S(1)} %collective-permute-done.26.c.refs_2_, ...), custom_call_target="tpu_custom_call" | custom-call | flops 4000000000 | bytes 1000000 | tf_op jit(solution)/shard_map/pallas_call | solution.py:273
  (82 shorter events, 33.4 us)
Async XLA Ops:
  2.2 6.5 %collective-permute-start = (bf16[32,1024]{1,0:T(8,128)(2,1)S(1)}, bf16[32,1024]{1,0:T(8,128)(2,1)S(1)}, u32[]{:S(2)}, u32[]{:S(2)}) collective-permute-start(bf16[32,1024]{1,0:T(8,128)(2,1)S(1)} %shard_map.127), channel_id=1, source_target_pairs={{0,16},{16,0},{32,48},{48,32},{64,80},{80,64},{96,112},{112,96},{1... | collective-permute-start | bytes 196616 | tf_op jit(solution)/shard_map/ppermute | solution.py:16
  8.7 6.3 %collective-permute-start.1 = (bf16[64,1024]{1,0:T(8,128)(2,1)S(1)}, bf16[64,1024]{1,0:T(8,128)(2,1)S(1)}, u32[]{:S(2)}, u32[]{:S(2)}) collective-permute-start(bf16[64,1024]{1,0:T(8,128)(2,1)S(1)} %pad_maximum_fusion), channel_id=1, source_target_pairs={{0,96},{16,112},{32,0},{48,16},{64,32},{80,48},{96,64},{112,80},{1... | collective-permute-start | bytes 393224 | tf_op jit(solution)/shard_map/ppermute | solution.py:21
  11.7 9.6 %collective-permute-start.3 = (bf16[64,1024]{1,0:T(8,128)(2,1)S(1)}, bf16[64,1024]{1,0:T(8,128)(2,1)S(1)}, u32[]{:S(2)}, u32[]{:S(2)}) collective-permute-start(bf16[64,1024]{1,0:T(8,128)(2,1)S(1)} %pad_maximum_fusion), channel_id=1, source_target_pairs={{0,32},{16,48},{32,64},{48,80},{64,96},{80,112},{96,0},{112,16},{1... | collective-permute-start | bytes 393224 | tf_op jit(solution)/shard_map/ppermute | solution.py:21
  11.7 8.8 %collective-permute-start.2 = (bf16[64,1024]{1,0:T(8,128)(2,1)S(1)}, bf16[64,1024]{1,0:T(8,128)(2,1)S(1)}, u32[]{:S(2)}, u32[]{:S(2)}) collective-permute-start(bf16[64,1024]{1,0:T(8,128)(2,1)S(1)} %pad_maximum_fusion), channel_id=1, source_target_pairs={{0,64},{16,80},{32,96},{48,112},{64,0},{80,16},{96,32},{112,48},{1... | collective-permute-start | bytes 393224 | tf_op jit(solution)/shard_map/ppermute | solution.py:21
  22.8 8.9 %collective-permute-start.10 = (bf16[64,2944]{1,0:T(8,128)(2,1)S(1)}, bf16[64,2944]{1,0:T(8,128)(2,1)S(1)}, u32[]{:S(2)}, u32[]{:S(2)}) collective-permute-start(bf16[64,2944]{1,0:T(8,128)(2,1)S(1)} %get-tuple-element.67), channel_id=1, source_target_pairs={{0,4},{1,5},{2,6},{3,7},{4,8},{5,9},{6,10},{7,11},{8,12},{9,13},{1... | collective-permute-start | bytes 1130504 | tf_op jit(solution)/shard_map/ppermute | solution.py:38
  24.5 7.6 %collective-permute-start.11 = (bf16[64,2944]{1,0:T(8,128)(2,1)S(1)}, bf16[64,2944]{1,0:T(8,128)(2,1)S(1)}, u32[]{:S(2)}, u32[]{:S(2)}) collective-permute-start(bf16[64,2944]{1,0:T(8,128)(2,1)S(1)} %get-tuple-element.68), channel_id=1, source_target_pairs={{0,12},{1,13},{2,14},{3,15},{4,0},{5,1},{6,2},{7,3},{8,4},{9,5},{1... | collective-permute-start | bytes 1130504 | tf_op jit(solution)/shard_map/ppermute | solution.py:38
  26.1 10.9 %collective-permute-start.12 = (bf16[64,2944]{1,0:T(8,128)(2,1)S(1)}, bf16[64,2944]{1,0:T(8,128)(2,1)S(1)}, u32[]{:S(2)}, u32[]{:S(2)}) collective-permute-start(bf16[64,2944]{1,0:T(8,128)(2,1)S(1)} %get-tuple-element.69), channel_id=1, source_target_pairs={{0,8},{1,9},{2,10},{3,11},{4,12},{5,13},{6,14},{7,15},{8,0},{9,1},... | collective-permute-start | bytes 1130504 | tf_op jit(solution)/shard_map/ppermute | solution.py:38
  37.1 9.0 %collective-permute-start.13 = (bf16[16,2944]{1,0:T(8,128)(2,1)S(1)}, bf16[16,2944]{1,0:T(8,128)(2,1)S(1)}, u32[]{:S(2)}, u32[]{:S(2)}) collective-permute-start(bf16[16,2944]{1,0:T(8,128)(2,1)S(1)} %get-tuple-element.71), channel_id=1, source_target_pairs={{0,1},{1,2},{2,3},{3,0},{4,5},{5,6},{6,7},{7,4},{8,9},{9,10},{10,1... | collective-permute-start | bytes 282632 | tf_op jit(solution)/shard_map/ppermute | solution.py:38
  40.3 25.0 %collective-permute-start.4 = (bf16[64,3072]{1,0:T(8,128)(2,1)S(1)}, bf16[64,3072]{1,0:T(8,128)(2,1)S(1)}, u32[]{:S(2)}, u32[]{:S(2)}) collective-permute-start(bf16[64,3072]{1,0:T(8,128)(2,1)S(1)} %get-tuple-element.59), channel_id=1, source_target_pairs={{0,4},{1,5},{2,6},{3,7},{4,8},{5,9},{6,10},{7,11},{8,12},{9,13},{1... | collective-permute-start | bytes 1179656 | tf_op jit(solution)/shard_map/ppermute | solution.py:38
  41.8 23.5 %collective-permute-start.5 = (bf16[64,3072]{1,0:T(8,128)(2,1)S(1)}, bf16[64,3072]{1,0:T(8,128)(2,1)S(1)}, u32[]{:S(2)}, u32[]{:S(2)}) collective-permute-start(bf16[64,3072]{1,0:T(8,128)(2,1)S(1)} %get-tuple-element.60), channel_id=1, source_target_pairs={{0,12},{1,13},{2,14},{3,15},{4,0},{5,1},{6,2},{7,3},{8,4},{9,5},{1... | collective-permute-start | bytes 1179656 | tf_op jit(solution)/shard_map/ppermute | solution.py:38
  43.6 21.7 %collective-permute-start.6 = (bf16[64,3072]{1,0:T(8,128)(2,1)S(1)}, bf16[64,3072]{1,0:T(8,128)(2,1)S(1)}, u32[]{:S(2)}, u32[]{:S(2)}) collective-permute-start(bf16[64,3072]{1,0:T(8,128)(2,1)S(1)} %get-tuple-element.61), channel_id=1, source_target_pairs={{0,8},{1,9},{2,10},{3,11},{4,12},{5,13},{6,14},{7,15},{8,0},{9,1},... | collective-permute-start | bytes 1179656 | tf_op jit(solution)/shard_map/ppermute | solution.py:38
  44.0 8.6 %collective-permute-start.14 = (bf16[16,2944]{1,0:T(8,128)(2,1)S(1)}, bf16[16,2944]{1,0:T(8,128)(2,1)S(1)}, u32[]{:S(2)}, u32[]{:S(2)}) collective-permute-start(bf16[16,2944]{1,0:T(8,128)(2,1)S(1)} %get-tuple-element.72), channel_id=1, source_target_pairs={{0,3},{1,0},{2,1},{3,2},{4,7},{5,4},{6,5},{7,6},{8,11},{9,8},{10,9... | collective-permute-start | bytes 282632 | tf_op jit(solution)/shard_map/ppermute | solution.py:38
  46.1 7.1 %collective-permute-start.15 = (bf16[16,2944]{1,0:T(8,128)(2,1)S(1)}, bf16[16,2944]{1,0:T(8,128)(2,1)S(1)}, u32[]{:S(2)}, u32[]{:S(2)}) collective-permute-start(bf16[16,2944]{1,0:T(8,128)(2,1)S(1)} %get-tuple-element.73), channel_id=1, source_target_pairs={{0,2},{1,3},{2,0},{3,1},{4,6},{5,7},{6,4},{7,5},{8,10},{9,11},{10,... | collective-permute-start | bytes 282632 | tf_op jit(solution)/shard_map/ppermute | solution.py:38
  53.4 5.9 %collective-permute-start.24 = (bf16[16,2944]{1,0:T(8,128)(2,1)S(1)}, bf16[16,2944]{1,0:T(8,128)(2,1)S(1)}, u32[]{:S(2)}, u32[]{:S(2)}) collective-permute-start(bf16[16,2944]{1,0:T(8,128)(2,1)S(1)} %shard_map.133.first.a), channel_id=1, source_target_pairs={{0,1},{1,2},{2,3},{3,0},{4,5},{5,6},{6,7},{7,4},{8,9},{9,10},{10,1... | collective-permute-start | bytes 282632 | tf_op jit(solution)/shard_map/ppermute | solution.py:38
  54.9 6.7 %collective-permute-start.23 = (bf16[16,2944]{1,0:T(8,128)(2,1)S(1)}, bf16[16,2944]{1,0:T(8,128)(2,1)S(1)}, u32[]{:S(2)}, u32[]{:S(2)}) collective-permute-start(bf16[16,2944]{1,0:T(8,128)(2,1)S(1)} %shard_map.133.first.a), channel_id=1, source_target_pairs={{0,2},{1,3},{2,0},{3,1},{4,6},{5,7},{6,4},{7,5},{8,10},{9,11},{10,... | collective-permute-start | bytes 282632 | tf_op jit(solution)/shard_map/ppermute | solution.py:38
  59.3 4.6 %collective-permute-start.22 = (bf16[16,2944]{1,0:T(8,128)(2,1)S(1)}, bf16[16,2944]{1,0:T(8,128)(2,1)S(1)}, u32[]{:S(2)}, u32[]{:S(2)}) collective-permute-start(bf16[16,2944]{1,0:T(8,128)(2,1)S(1)} %shard_map.133.first.a), channel_id=1, source_target_pairs={{0,3},{1,0},{2,1},{3,2},{4,7},{5,4},{6,5},{7,6},{8,11},{9,8},{10,9... | collective-permute-start | bytes 282632 | tf_op jit(solution)/shard_map/ppermute | solution.py:38
  63.9 24.7 %collective-permute-start.27 = (bf16[64,2944]{1,0:T(8,128)(2,1)S(1)}, bf16[64,2944]{1,0:T(8,128)(2,1)S(1)}, u32[]{:S(2)}, u32[]{:S(2)}) collective-permute-start(bf16[64,2944]{1,0:T(8,128)(2,1)S(1)} %shard_map.136.a.refs_0_), channel_id=1, source_target_pairs={{0,4},{1,5},{2,6},{3,7},{4,8},{5,9},{6,10},{7,11},{8,12},{9,13},{1... | collective-permute-start | bytes 1130504 | tf_op jit(solution)/shard_map/ppermute | solution.py:38
  65.5 5.9 %collective-permute-start.7 = (bf16[16,3072]{1,0:T(8,128)(2,1)S(1)}, bf16[16,3072]{1,0:T(8,128)(2,1)S(1)}, u32[]{:S(2)}, u32[]{:S(2)}) collective-permute-start(bf16[16,3072]{1,0:T(8,128)(2,1)S(1)} %get-tuple-element.63), channel_id=1, source_target_pairs={{0,1},{1,2},{2,3},{3,0},{4,5},{5,6},{6,7},{7,4},{8,9},{9,10},{10,1... | collective-permute-start | bytes 294920 | tf_op jit(solution)/shard_map/ppermute | solution.py:38
  65.7 5.7 %collective-permute-start.8 = (bf16[16,3072]{1,0:T(8,128)(2,1)S(1)}, bf16[16,3072]{1,0:T(8,128)(2,1)S(1)}, u32[]{:S(2)}, u32[]{:S(2)}) collective-permute-start(bf16[16,3072]{1,0:T(8,128)(2,1)S(1)} %get-tuple-element.64), channel_id=1, source_target_pairs={{0,3},{1,0},{2,1},{3,2},{4,7},{5,4},{6,5},{7,6},{8,11},{9,8},{10,9... | collective-permute-start | bytes 294920 | tf_op jit(solution)/shard_map/ppermute | solution.py:38
  68.9 6.1 %collective-permute-start.9 = (bf16[16,3072]{1,0:T(8,128)(2,1)S(1)}, bf16[16,3072]{1,0:T(8,128)(2,1)S(1)}, u32[]{:S(2)}, u32[]{:S(2)}) collective-permute-start(bf16[16,3072]{1,0:T(8,128)(2,1)S(1)} %get-tuple-element.65), channel_id=1, source_target_pairs={{0,2},{1,3},{2,0},{3,1},{4,6},{5,7},{6,4},{7,5},{8,10},{9,11},{10,... | collective-permute-start | bytes 294920 | tf_op jit(solution)/shard_map/ppermute | solution.py:38
  75.3 7.3 %collective-permute-start.18 = (bf16[16,3072]{1,0:T(8,128)(2,1)S(1)}, bf16[16,3072]{1,0:T(8,128)(2,1)S(1)}, u32[]{:S(2)}, u32[]{:S(2)}) collective-permute-start(bf16[16,3072]{1,0:T(8,128)(2,1)S(1)} %shard_map.134.a), channel_id=1, source_target_pairs={{0,1},{1,2},{2,3},{3,0},{4,5},{5,6},{6,7},{7,4},{8,9},{9,10},{10,1... | collective-permute-start | bytes 294920 | tf_op jit(solution)/shard_map/ppermute | solution.py:38
  75.7 8.8 %collective-permute-start.17 = (bf16[16,3072]{1,0:T(8,128)(2,1)S(1)}, bf16[16,3072]{1,0:T(8,128)(2,1)S(1)}, u32[]{:S(2)}, u32[]{:S(2)}) collective-permute-start(bf16[16,3072]{1,0:T(8,128)(2,1)S(1)} %shard_map.134.a), channel_id=1, source_target_pairs={{0,2},{1,3},{2,0},{3,1},{4,6},{5,7},{6,4},{7,5},{8,10},{9,11},{10,... | collective-permute-start | bytes 294920 | tf_op jit(solution)/shard_map/ppermute | solution.py:38
  78.8 6.4 %collective-permute-start.16 = (bf16[16,3072]{1,0:T(8,128)(2,1)S(1)}, bf16[16,3072]{1,0:T(8,128)(2,1)S(1)}, u32[]{:S(2)}, u32[]{:S(2)}) collective-permute-start(bf16[16,3072]{1,0:T(8,128)(2,1)S(1)} %shard_map.134.a), channel_id=1, source_target_pairs={{0,3},{1,0},{2,1},{3,2},{4,7},{5,4},{6,5},{7,6},{8,11},{9,8},{10,9... | collective-permute-start | bytes 294920 | tf_op jit(solution)/shard_map/ppermute | solution.py:38
  79.4 10.8 %collective-permute-start.26 = (bf16[64,2944]{1,0:T(8,128)(2,1)S(1)}, bf16[64,2944]{1,0:T(8,128)(2,1)S(1)}, u32[]{:S(2)}, u32[]{:S(2)}) collective-permute-start(bf16[64,2944]{1,0:T(8,128)(2,1)S(1)} %shard_map.136.a.refs_0_), channel_id=1, source_target_pairs={{0,8},{1,9},{2,10},{3,11},{4,12},{5,13},{6,14},{7,15},{8,0},{9,1},... | collective-permute-start | bytes 1130504 | tf_op jit(solution)/shard_map/ppermute | solution.py:38
  82.6 8.9 %collective-permute-start.25 = (bf16[64,2944]{1,0:T(8,128)(2,1)S(1)}, bf16[64,2944]{1,0:T(8,128)(2,1)S(1)}, u32[]{:S(2)}, u32[]{:S(2)}) collective-permute-start(bf16[64,2944]{1,0:T(8,128)(2,1)S(1)} %shard_map.136.a.refs_0_), channel_id=1, source_target_pairs={{0,12},{1,13},{2,14},{3,15},{4,0},{5,1},{6,2},{7,3},{8,4},{9,5},{1... | collective-permute-start | bytes 1130504 | tf_op jit(solution)/shard_map/ppermute | solution.py:38
  85.2 9.1 %collective-permute-start.21 = (bf16[64,3072]{1,0:T(8,128)(2,1)S(1)}, bf16[64,3072]{1,0:T(8,128)(2,1)S(1)}, u32[]{:S(2)}, u32[]{:S(2)}) collective-permute-start(bf16[64,3072]{1,0:T(8,128)(2,1)S(1)} %shard_map.135.a.refs_4_), channel_id=1, source_target_pairs={{0,4},{1,5},{2,6},{3,7},{4,8},{5,9},{6,10},{7,11},{8,12},{9,13},{1... | collective-permute-start | bytes 1179656 | tf_op jit(solution)/shard_map/ppermute | solution.py:38
  86.6 12.0 %collective-permute-start.20 = (bf16[64,3072]{1,0:T(8,128)(2,1)S(1)}, bf16[64,3072]{1,0:T(8,128)(2,1)S(1)}, u32[]{:S(2)}, u32[]{:S(2)}) collective-permute-start(bf16[64,3072]{1,0:T(8,128)(2,1)S(1)} %shard_map.135.a.refs_4_), channel_id=1, source_target_pairs={{0,8},{1,9},{2,10},{3,11},{4,12},{5,13},{6,14},{7,15},{8,0},{9,1},... | collective-permute-start | bytes 1179656 | tf_op jit(solution)/shard_map/ppermute | solution.py:38
  88.6 11.4 %collective-permute-start.19 = (bf16[64,3072]{1,0:T(8,128)(2,1)S(1)}, bf16[64,3072]{1,0:T(8,128)(2,1)S(1)}, u32[]{:S(2)}, u32[]{:S(2)}) collective-permute-start(bf16[64,3072]{1,0:T(8,128)(2,1)S(1)} %shard_map.135.a.refs_4_), channel_id=1, source_target_pairs={{0,12},{1,13},{2,14},{3,15},{4,0},{5,1},{6,2},{7,3},{8,4},{9,5},{1... | collective-permute-start | bytes 1179656 | tf_op jit(solution)/shard_map/ppermute | solution.py:38
  101.7 1.7 %collective-permute-start.28 = (bf16[4,32,1280]{2,1,0:T(8,128)(2,1)S(1)}, bf16[4,32,1280]{2,1,0:T(8,128)(2,1)S(1)}, u32[]{:S(2)}, u32[]{:S(2)}) collective-permute-start(bf16[4,32,1280]{2,1,0:T(8,128)(2,1)S(1)} %get-tuple-element.78), channel_id=1, source_target_pairs={{0,16},{16,0},{32,48},{48,32},{64,80},{80,64},{96,112},{112,96},{1... | collective-permute-start | bytes 983048 | tf_op jit(solution)/shard_map/ppermute | solution.py:16
  103.5 6.5 %collective-permute-start.29 = (bf16[32,1792]{1,0:T(8,128)(2,1)S(1)}, bf16[32,1792]{1,0:T(8,128)(2,1)S(1)}, u32[]{:S(2)}, u32[]{:S(2)}) collective-permute-start(bf16[32,1792]{1,0:T(8,128)(2,1)S(1)} %get-tuple-element.81), channel_id=1, source_target_pairs={{0,32},{16,48},{32,64},{48,80},{64,96},{80,112},{96,0},{112,16},{1... | collective-permute-start | bytes 344072 | tf_op jit(solution)/shard_map/ppermute | solution.py:21
  103.6 8.1 %collective-permute-start.30 = (bf16[32,1792]{1,0:T(8,128)(2,1)S(1)}, bf16[32,1792]{1,0:T(8,128)(2,1)S(1)}, u32[]{:S(2)}, u32[]{:S(2)}) collective-permute-start(bf16[32,1792]{1,0:T(8,128)(2,1)S(1)} %get-tuple-element.82), channel_id=1, source_target_pairs={{0,96},{16,112},{32,0},{48,16},{64,32},{80,48},{96,64},{112,80},{1... | collective-permute-start | bytes 344072 | tf_op jit(solution)/shard_map/ppermute | solution.py:21
  106.8 6.3 %collective-permute-start.31 = (bf16[32,1792]{1,0:T(8,128)(2,1)S(1)}, bf16[32,1792]{1,0:T(8,128)(2,1)S(1)}, u32[]{:S(2)}, u32[]{:S(2)}) collective-permute-start(bf16[32,1792]{1,0:T(8,128)(2,1)S(1)} %get-tuple-element.83), channel_id=1, source_target_pairs={{0,64},{16,80},{32,96},{48,112},{64,0},{80,16},{96,32},{112,48},{1... | collective-permute-start | bytes 344072 | tf_op jit(solution)/shard_map/ppermute | solution.py:21
  (13 other events, 159.8 us)
